TPU v7x, 32 devices: a whole 2x2x4 slice. The times are simulated.
32 devices in a mesh: seq: 8 (over z, core), mp: 4 (over y, x).
Axes of the slice: x: 2, y: 2, z: 4, core: 2. Of those that a mesh axis runs over, the one named last changes fastest.
Arguments:
- hidden_in: bfloat16 [4096, 4096], P('seq', 'mp'), may hold values from -30 to 30
- norm_gain: float32 [4096], replicated, may hold values from 0.1 to 1.9
- w_z: bfloat16 [4096, 8192], P('seq', 'mp'), may hold values from -0.09375 to 0.09375
- w_x: bfloat16 [4096, 8192], P('seq', 'mp'), may hold values from -0.09375 to 0.09375
- w_b: bfloat16 [4096, 1024], P('seq', 'mp'), may hold values from -0.09375 to 0.09375
- w_c: bfloat16 [4096, 1024], P('seq', 'mp'), may hold values from -0.09375 to 0.09375
- w_dt: bfloat16 [4096, 128], P('seq', 'mp'), may hold values from -0.0625 to 0.0625
- conv_x: float32 [4, 8192], P(None, 'mp'), may hold values from -3 to 3
- conv_b: float32 [4, 1024], P(None, 'mp'), may hold values from -3 to 3
- conv_c: float32 [4, 1024], P(None, 'mp'), may hold values from -3 to 3
- dt_bias: float32 [128], P('mp'), may hold values from -9 to -5
- a_rate: float32 [128], P('mp'), may hold values from 0.5 to 16
- skip_gain: float32 [128], P('mp'), may hold values from -3 to 3
- group_gain: float32 [8192], P('mp'), may hold values from 0.1 to 1.9
- w_out: bfloat16 [8192, 4096], P('mp', 'seq'), may hold values from -0.0625 to 0.0625
- attn_gain: float32 [4096], replicated, may hold values from 0.1 to 1.9
- w_q: bfloat16 [4096, 4096], P(None, 'mp'), may hold values from -0.125 to 0.125
- w_k: bfloat16 [4096, 1024], P(None, 'mp'), may hold values from -0.125 to 0.125
- w_v: bfloat16 [4096, 1024], P(None, 'mp'), may hold values from -0.09375 to 0.09375
Outputs:
- mixed: float32 [4096, 4096], P('seq', 'mp')
- context: float32 [4096, 4096], P('seq', 'mp')
All inputs are finite; a program needn't handle non-finite values.
Results may differ from a plain program's by a relative error of at most 0.017.
Values may be sent and summed in bfloat16 or wider, within the bound.
A program may use at most 192 MiB of HBM per device.

v0:
```python
import functools
import math

import jax
import jax.numpy as jnp
from jax import lax
from jax.experimental import pallas as pl
from jax.experimental.pallas import tpu as pltpu
from jax.sharding import PartitionSpec as P

P_SIZE = 64
N = 128
HD = 128
WINDOW = 4096
QB = 128
LANES = 128
VMEM_LIMIT = 62 * 1024 * 1024

HIGH = lax.Precision.HIGHEST
F32 = jnp.float32
BF16 = jnp.bfloat16


def from_behind(block, axis, distance):
    devices = range(lax.axis_size(axis))
    route = [(i - distance, i) for i in devices if i - distance in devices]
    return lax.ppermute(block, axis, route)


def rms_norm(values, gain):
    return values * lax.rsqrt(jnp.mean(values * values, axis=-1, keepdims=True) + 1e-05) * gain


def signal_seq(sem, index):
    pl.semaphore_signal(
        sem, inc=1, device_id={"seq": index}, device_id_type=pl.DeviceIdType.MESH
    )


def signal_mp(sem, index):
    pl.semaphore_signal(
        sem, inc=1, device_id={"mp": index}, device_id_type=pl.DeviceIdType.MESH
    )


def norm_rows(source, gain_ref, target):
    rows = source.shape[0]
    tile = min(64, rows)

    def body(i, carry_none):
        here = pl.ds(pl.multiple_of(i * tile, tile), tile)
        target[here, :] = rms_norm(source[here, :].astype(F32), gain_ref[...]).astype(BF16)
        return carry_none

    lax.fori_loop(0, rows // tile, body, 0)


def share_features(m, source, whole, send_sem, recv_sem):
    member = lax.axis_index("mp")
    wide = source.shape[1]
    own = pl.ds(pl.multiple_of(member * wide, wide), wide)
    copies = [
        pltpu.make_async_remote_copy(
            src_ref=source,
            dst_ref=whole.at[:, own],
            send_sem=send_sem.at[d - 1],
            recv_sem=recv_sem.at[d - 1],
            device_id={"mp": lax.rem(member + d, m)},
            device_id_type=pl.DeviceIdType.MESH,
        )
        for d in range(1, m)
    ]
    for copy in copies:
        copy.start()
    return copies, own


def features_arrived(m, whole, wide, recv_sem):
    member = lax.axis_index("mp")
    for d in range(1, m):
        sender = lax.rem(member - d + m, m)
        there = whole.at[:, pl.ds(pl.multiple_of(sender * wide, wide), wide)]
        pltpu.make_async_copy(there, there, recv_sem.at[d - 1]).wait()


def gather_dot_kernel(
    n,
    m,
    hidden_ref,
    gain_ref,
    w_ref,
    out_ref,
    slots,
    normed_ref,
    local_sem,
    send_sem,
    recv_sem,
    own_sem,
    mp_send_sem,
    mp_recv_sem,
):
    me = lax.axis_index("seq")
    member = lax.axis_index("mp")
    ring = n // 2
    half = ring // 2
    chip, core = me // 2, lax.rem(me, 2)
    up = lax.rem(chip + 1, ring) * 2 + core
    down = lax.rem(chip + ring - 1, ring) * 2 + core
    partner = chip * 2 + 1 - core
    depth, cols = w_ref.shape
    mid = depth // 2

    barrier = pltpu.get_barrier_semaphore()
    for other in (up, down, partner):
        signal_seq(barrier, other)
    for d in range(1, m):
        signal_mp(barrier, lax.rem(member + d, m))
    pl.semaphore_wait(barrier, 3 + m - 1)

    shared, own = share_features(m, hidden_ref, normed_ref, mp_send_sem, mp_recv_sem)
    own_copy = pltpu.make_async_copy(hidden_ref, normed_ref.at[:, own], own_sem)
    own_copy.start()
    local = pltpu.make_async_copy(w_ref, slots.at[0], local_sem)
    local.start()
    started = []

    def send(source, slot, rows, part, target):
        copy = pltpu.make_async_remote_copy(
            src_ref=source,
            dst_ref=slots.at[slot, rows],
            send_sem=send_sem.at[len(started)],
            recv_sem=recv_sem.at[2 * slot + part],
            device_id={"seq": target},
            device_id_type=pl.DeviceIdType.MESH,
        )
        copy.start()
        started.append(copy)

    def arrived(slot, rows, part):
        pltpu.make_async_copy(
            slots.at[slot, rows], slots.at[slot, rows], recv_sem.at[2 * slot + part]
        ).wait()

    whole, upper, lower = pl.ds(0, depth), pl.ds(0, mid), pl.ds(mid, mid)
    send(w_ref, 2 * 1, whole, 0, up)
    send(w_ref, 2 * (ring - 1), whole, 0, down)
    send(w_ref, 1, whole, 0, partner)

    def multiply(slot, first=False):
        step, lane = slot // 2, slot % 2
        origin = lax.rem(chip - step + ring, ring) * 2
        owner = origin + (core if lane == 0 else 1 - core)
        features = pl.ds(pl.multiple_of(owner * depth, depth), depth)

        def tile(start, width):
            where = pl.ds(start, width)
            product = jnp.dot(
                normed_ref[:, features], slots[slot, :, where], preferred_element_type=F32
            )
            if first:
                out_ref[:, where] = product
            else:
                out_ref[:, where] += product

        width = 512
        full = cols // width

        def body(i, carry):
            tile(pl.multiple_of(i * width, width), width)
            return carry

        lax.fori_loop(0, full, body, 0)
        if cols % width:
            tile(full * width, cols % width)

    own_copy.wait()
    features_arrived(m, normed_ref, hidden_ref.shape[1], mp_recv_sem)
    norm_rows(normed_ref, gain_ref, normed_ref)
    local.wait()
    multiply(0, True)
    arrived(1, whole, 0)
    multiply(1)
    for d in range(1, half):
        s_up, s_down = 2 * d, 2 * (ring - d)
        last = d + 1 == half
        arrived(s_up, whole, 0)
        rows = upper if last else whole
        send(slots.at[s_up, rows], 2 * (d + 1), rows, 0, up)
        arrived(s_down, whole, 0)
        rows = lower if last else whole
        send(slots.at[s_down, rows], 2 * (ring - d - 1), rows, 1 if last else 0, down)
        send(slots.at[s_up, whole], s_up + 1, whole, 0, partner)
        send(slots.at[s_down, whole], s_down + 1, whole, 0, partner)
        multiply(s_up)
        multiply(s_down)
        arrived(s_up + 1, whole, 0)
        multiply(s_up + 1)
        arrived(s_down + 1, whole, 0)
        multiply(s_down + 1)
    far = 2 * half
    arrived(far, upper, 0)
    send(slots.at[far, upper], far + 1, upper, 0, partner)
    arrived(far, lower, 1)
    send(slots.at[far, lower], far + 1, lower, 1, partner)
    multiply(far)
    arrived(far + 1, upper, 0)
    arrived(far + 1, lower, 1)
    multiply(far + 1)
    for copy in started + shared:
        copy.wait_send()


def gather_dot(hidden, gain, weights):
    n, m = lax.axis_size("seq"), lax.axis_size("mp")
    depth, cols = weights.shape
    rows, features = hidden.shape[0], hidden.shape[1] * m
    ring = n // 2
    sends = 3 + 4 * (ring // 2 - 1) + 2
    return pl.pallas_call(
        functools.partial(gather_dot_kernel, n, m),
        out_shape=jax.ShapeDtypeStruct((rows, cols), F32),
        in_specs=[
            pl.BlockSpec(memory_space=pl.ANY),
            pl.BlockSpec(memory_space=pltpu.VMEM),
            pl.BlockSpec(memory_space=pl.ANY),
        ],
        out_specs=pl.BlockSpec(memory_space=pltpu.VMEM),
        scratch_shapes=[
            pltpu.VMEM((n, depth, cols), BF16),
            pltpu.VMEM((rows, features), BF16),
            pltpu.SemaphoreType.DMA,
            pltpu.SemaphoreType.DMA((sends,)),
            pltpu.SemaphoreType.DMA((2 * n,)),
            pltpu.SemaphoreType.DMA,
            pltpu.SemaphoreType.DMA((m - 1,)),
            pltpu.SemaphoreType.DMA((m - 1,)),
        ],
        compiler_params=pltpu.CompilerParams(
            collective_id=0, has_side_effects=True, vmem_limit_bytes=VMEM_LIMIT
        ),
        cost_estimate=pl.CostEstimate(
            flops=2 * rows * features * cols,
            bytes_accessed=160_000_000,
            transcendentals=0,
        ),
    )(hidden, gain, weights)


def silu(v):
    return v / (1.0 + jnp.exp(-v))


def spread_heads(values, expand):
    high = values.astype(BF16)
    low = (values - high.astype(F32)).astype(BF16)
    return jnp.dot(high, expand, preferred_element_type=F32) + jnp.dot(
        low, expand, preferred_element_type=F32
    )


def mixer_kernel(
    n,
    heads,
    groups,
    proj_ref,
    rim_ref,
    taps_ref,
    bias_ref,
    rate_ref,
    skip_ref,
    gain_ref,
    expand_ref,
    y_ref,
    window,
    conv,
    ssd,
    reads,
    logs,
    state,
    carry,
    state_out,
    state_in,
    send_sem,
    recv_sem,
):
    me = lax.axis_index("seq")
    rows = proj_ref.shape[0]
    inner = heads * P_SIZE
    width = inner + 2 * groups * N
    gate_at = width + LANES
    per_group = inner // groups
    blocks = rows // QB
    kw = taps_ref.shape[0]

    barrier = pltpu.get_barrier_semaphore()
    signal_seq(barrier, lax.rem(me + 1, n))
    signal_seq(barrier, lax.rem(me + n - 1, n))
    pl.semaphore_wait(barrier, 2)

    expand = expand_ref[...]
    window[0:8, :] = rim_ref[...]
    state[...] = jnp.zeros_like(state)
    carry[...] = jnp.zeros_like(carry)
    row_id = lax.broadcasted_iota(jnp.int32, (QB, QB), 0)
    col_id = lax.broadcasted_iota(jnp.int32, (QB, QB), 1)
    causal = row_id >= col_id
    low_lanes = col_id < P_SIZE
    tri = jnp.where(causal, 1.0, 0.0).astype(F32)

    def block(i, carry_none):
        base = pl.multiple_of(i * QB, QB)
        here = pl.ds(base, QB)
        window[8 : 8 + QB, :] = proj_ref[here, 0:width]
        step_cols = 256 if width % 256 == 0 else 128
        for at in range(0, width, step_cols):
            cs = slice(at, at + step_cols)
            total = None
            for j in range(kw):
                term = taps_ref[j : j + 1, cs] * window[8 - kw + 1 + j : 8 - kw + 1 + j + QB, cs]
                total = term if total is None else total + term
            conv[:, cs] = silu(total)
        window[0:8, :] = window[QB : QB + 8, :]

        raw = proj_ref[here, width : width + LANES] + bias_ref[...]
        steps = jnp.maximum(raw, 0.0) + jnp.log1p(jnp.exp(-jnp.abs(raw)))
        decays = -rate_ref[...] * steps
        cum = jnp.dot(tri, decays, precision=HIGH, preferred_element_type=F32)
        cum_t = jnp.transpose(cum)
        logs[here, :] = cum + carry[0:1, :]
        carry[...] = carry[...] + cum[QB - 1 : QB, :]
        grown = jnp.exp(cum)
        tail = jnp.exp(cum[QB - 1 : QB, :] - cum)

        for g in range(groups):
            lanes = slice(g * per_group, (g + 1) * per_group)
            expand_g = expand[:, lanes]
            x = conv[:, lanes]
            b = conv[:, inner + g * N : inner + (g + 1) * N].astype(BF16)
            c = conv[:, inner + (groups + g) * N : inner + (groups + g + 1) * N].astype(BF16)
            reads[here, g * N : (g + 1) * N] = c
            scaled = x * spread_heads(steps, expand_g)
            grown_e = spread_heads(grown, expand_g)
            tailed = (scaled * spread_heads(tail, expand_g)).astype(BF16)
            scaled_low = scaled.astype(BF16)
            held = state[:, lanes]
            carried = grown_e * jnp.dot(c, held.astype(BF16), preferred_element_type=F32)
            ssd[here, lanes] = carried + skip_ref[:, lanes] * x
            fresh = lax.dot_general(
                b, tailed, (((0,), (0,)), ((), ())), preferred_element_type=F32
            )
            state[:, lanes] = grown_e[QB - 1 : QB, :] * held + fresh
            affinity = lax.dot_general(
                c, b, (((1,), (1,)), ((), ())), preferred_element_type=F32
            )
            affinity = jnp.where(causal, affinity, 0.0)
            for pair in range(per_group // LANES):
                at = pair * LANES
                inputs = scaled_low[:, at : at + LANES]
                outs = []
                for k in range(2):
                    h = (g * per_group + at) // P_SIZE + k
                    spread = jnp.minimum(cum[:, h : h + 1] - cum_t[h : h + 1, :], 0.0)
                    mixing = (affinity * jnp.exp(spread)).astype(BF16)
                    outs.append(jnp.dot(mixing, inputs, preferred_element_type=F32))
                where = slice(g * per_group + at, g * per_group + at + LANES)
                ssd[here, where] += jnp.where(low_lanes, outs[0], outs[1])
        return carry_none

    lax.fori_loop(0, blocks, block, 0)

    parts = 4
    piece = inner // parts
    decay = jnp.exp(carry[...])

    def hand_on(k):
        lanes = slice(k * piece, (k + 1) * piece)
        return pltpu.make_async_remote_copy(
            src_ref=state_out.at[:, lanes],
            dst_ref=state_in.at[:, lanes],
            send_sem=send_sem.at[k],
            recv_sem=recv_sem.at[k],
            device_id={"seq": jnp.minimum(me + 1, n - 1)},
            device_id_type=pl.DeviceIdType.MESH,
        )

    for k in range(parts):
        lanes = slice(k * piece, (k + 1) * piece)
        weight = spread_heads(decay, expand[:, lanes])[0:1, :]

        @pl.when(me > 0)
        def _():
            hand_on(k).wait_recv()
            before = state_in[:, lanes].astype(F32)
            state_out[:, lanes] = (weight * before + state[:, lanes]).astype(BF16)

        @pl.when(me == 0)
        def _():
            state_out[:, lanes] = state[:, lanes].astype(BF16)
            state_in[:, lanes] = jnp.zeros((N, piece), BF16)

        @pl.when(me < n - 1)
        def _():
            hand_on(k).start()

    def finish(i, carry_none):
        here = pl.ds(pl.multiple_of(i * QB, QB), QB)
        grown = jnp.exp(logs[here, :])
        for g in range(groups):
            lanes = slice(g * per_group, (g + 1) * per_group)
            late = jnp.dot(
                reads[here, g * N : (g + 1) * N],
                state_in[:, lanes],
                preferred_element_type=F32,
            )
            full = ssd[here, lanes] + spread_heads(grown, expand[:, lanes]) * late
            gate = proj_ref[here, gate_at + g * per_group : gate_at + (g + 1) * per_group]
            gated = full * silu(gate)
            power = jnp.mean(gated * gated, axis=-1, keepdims=True)
            y_ref[here, lanes] = (gated * lax.rsqrt(power + 1e-05) * gain_ref[:, lanes]).astype(BF16)
        return carry_none

    lax.fori_loop(0, blocks, finish, 0)

    @pl.when(me < n - 1)
    def _():
        for k in range(parts):
            hand_on(k).wait_send()


def mixer(proj, rim, taps, bias, rate, skip, gain, heads, groups):
    n = lax.axis_size("seq")
    rows = proj.shape[0]
    inner = heads * P_SIZE
    width = inner + 2 * groups * N
    expand = (
        jnp.arange(LANES)[:, None] == (jnp.arange(inner) // P_SIZE)[None, :]
    ).astype(BF16)
    vmem = pl.BlockSpec(memory_space=pltpu.VMEM)
    return pl.pallas_call(
        functools.partial(mixer_kernel, n, heads, groups),
        out_shape=jax.ShapeDtypeStruct((rows, inner), BF16),
        in_specs=[vmem] * 8,
        out_specs=vmem,
        scratch_shapes=[
            pltpu.VMEM((8 + QB, width), F32),
            pltpu.VMEM((QB, width), F32),
            pltpu.VMEM((rows, inner), F32),
            pltpu.VMEM((rows, groups * N), BF16),
            pltpu.VMEM((rows, LANES), F32),
            pltpu.VMEM((N, inner), F32),
            pltpu.VMEM((8, LANES), F32),
            pltpu.VMEM((N, inner), BF16),
            pltpu.VMEM((N, inner), BF16),
            pltpu.SemaphoreType.DMA((4,)),
            pltpu.SemaphoreType.DMA((4,)),
        ],
        compiler_params=pltpu.CompilerParams(
            collective_id=1, has_side_effects=True, vmem_limit_bytes=48 * 1024 * 1024
        ),
        cost_estimate=pl.CostEstimate(
            flops=8_000_000_000, bytes_accessed=100_000_000, transcendentals=8_000_000
        ),
    )(proj, rim, taps, bias, rate, skip, gain, expand)


def output_kernel(
    m,
    y_ref,
    w_ref,
    hidden_ref,
    gain_ref,
    mixed_ref,
    normed_ref,
    outgoing,
    incoming,
    low,
    part_send,
    part_recv,
    own_sem,
    mp_send,
    mp_recv,
):
    member = lax.axis_index("mp")
    wide = hidden_ref.shape[1]
    barrier = pltpu.get_barrier_semaphore()
    for d in range(1, m):
        signal_mp(barrier, lax.rem(member + d, m))
    pl.semaphore_wait(barrier, m - 1)
    tile = min(512, wide)

    def part(target, store):
        for at in range(0, wide, tile):
            where = pl.ds(pl.multiple_of(target * wide + at, tile), tile)
            term = jnp.dot(y_ref[...], w_ref[:, where], preferred_element_type=F32)
            store(slice(at, at + tile), term.astype(BF16))

    copies = []
    for d in range(1, m):
        target = lax.rem(member + d, m)

        def keep(where, term):
            outgoing[d - 1, :, where] = term

        part(target, keep)
        copy = pltpu.make_async_remote_copy(
            src_ref=outgoing.at[d - 1],
            dst_ref=incoming.at[d - 1],
            send_sem=part_send.at[d - 1],
            recv_sem=part_recv.at[d - 1],
            device_id={"mp": target},
            device_id_type=pl.DeviceIdType.MESH,
        )
        copy.start()
        copies.append(copy)

    def begin(where, term):
        mixed_ref[:, where] = hidden_ref[:, where].astype(F32) + term.astype(F32)

    part(member, begin)
    for d in range(1, m):
        copies[d - 1].wait_recv()
        if d < m - 1:
            mixed_ref[...] += incoming[d - 1].astype(F32)
        else:
            total = mixed_ref[...] + incoming[d - 1].astype(F32)
            mixed_ref[...] = total
            low[...] = total.astype(BF16)
    shared, own = share_features(m, low, normed_ref, mp_send, mp_recv)
    own_copy = pltpu.make_async_copy(low, normed_ref.at[:, own], own_sem)
    own_copy.start()
    own_copy.wait()
    features_arrived(m, normed_ref, wide, mp_recv)
    norm_rows(normed_ref, gain_ref, normed_ref)
    for copy in copies + shared:
        copy.wait_send()


def output_stage(y, weights, hidden, gain):
    m = lax.axis_size("mp")
    rows, wide = hidden.shape
    vmem = pl.BlockSpec(memory_space=pltpu.VMEM)
    return pl.pallas_call(
        functools.partial(output_kernel, m),
        out_shape=(
            jax.ShapeDtypeStruct((rows, wide), F32),
            jax.ShapeDtypeStruct((rows, wide * m), BF16),
        ),
        in_specs=[vmem] * 4,
        out_specs=(vmem, vmem),
        scratch_shapes=[
            pltpu.VMEM((m - 1, rows, wide), BF16),
            pltpu.VMEM((m - 1, rows, wide), BF16),
            pltpu.VMEM((rows, wide), BF16),
            pltpu.SemaphoreType.DMA((m - 1,)),
            pltpu.SemaphoreType.DMA((m - 1,)),
            pltpu.SemaphoreType.DMA,
            pltpu.SemaphoreType.DMA((m - 1,)),
            pltpu.SemaphoreType.DMA((m - 1,)),
        ],
        compiler_params=pltpu.CompilerParams(
            collective_id=2, has_side_effects=True, vmem_limit_bytes=56 * 1024 * 1024
        ),
        cost_estimate=pl.CostEstimate(
            flops=2 * rows * y.shape[1] * wide * m, bytes_accessed=60_000_000, transcendentals=0
        ),
    )(y, weights, hidden, gain)


def attention_kernel(n, rows, q_ref, k_ref, v_ref, o_ref, peak, total, acc):
    me = lax.axis_index("seq")
    reach = WINDOW // rows
    factor = HD ** (-0.5) * math.log2(math.e)
    query = q_ref[...]
    row_id = lax.broadcasted_iota(jnp.int32, (rows, rows), 0)
    col_id = lax.broadcasted_iota(jnp.int32, (rows, rows), 1)

    def visit(block, allowed, first, count=1):
        here = pl.ds(pl.multiple_of(block * rows, rows), count * rows)
        scores = lax.dot_general(
            query, k_ref[here, :], (((1,), (1,)), ((), ())), preferred_element_type=F32
        )
        if allowed is not None:
            scores = jnp.where(allowed, scores, -1e30)
        top = jnp.max(scores, axis=1, keepdims=True)
        if not first:
            before = peak[...]
            top = jnp.maximum(before, top)
        weights = jnp.exp2((scores - top) * factor)
        added = jnp.sum(weights, axis=1, keepdims=True)
        product = jnp.dot(weights.astype(BF16), v_ref[here, :], preferred_element_type=F32)
        if first:
            total[...] = added
            acc[...] = product
        else:
            shrink = jnp.exp2((before - top) * factor)
            total[...] = total[...] * shrink + added
            acc[...] = acc[...] * shrink + product
        peak[...] = top

    visit(me, row_id >= col_id, True)
    lowest = jnp.maximum(me - reach + 1, 0)

    twos = (me - lowest) // 2

    def body(i, carry_none):
        visit(lowest + 2 * i, None, False, 2)
        return carry_none

    lax.fori_loop(0, twos, body, 0)

    @pl.when(lowest + 2 * twos < me)
    def _():
        visit(me - 1, None, False)

    if n > reach:

        @pl.when(me >= reach)
        def _():
            visit(me - reach, col_id > row_id, False)

    o_ref[...] = acc[...] / total[...]


def attention(queries, pairs, kv_heads):
    n = lax.axis_size("seq")
    rows = queries.shape[0]
    keys = pairs.shape[0]
    per_kv = queries.shape[1] // HD // kv_heads
    return pl.pallas_call(
        functools.partial(attention_kernel, n, rows),
        grid=(kv_heads, per_kv),
        out_shape=jax.ShapeDtypeStruct(queries.shape, F32),
        in_specs=[
            pl.BlockSpec((rows, HD), lambda i, j: (0, i * per_kv + j)),
            pl.BlockSpec((keys, HD), lambda i, j: (0, i)),
            pl.BlockSpec((keys, HD), lambda i, j: (0, kv_heads + i)),
        ],
        out_specs=pl.BlockSpec((rows, HD), lambda i, j: (0, i * per_kv + j)),
        scratch_shapes=[
            pltpu.VMEM((rows, 1), F32),
            pltpu.VMEM((rows, 1), F32),
            pltpu.VMEM((rows, HD), F32),
        ],
        compiler_params=pltpu.CompilerParams(
            dimension_semantics=("arbitrary", "arbitrary"), vmem_limit_bytes=40 * 1024 * 1024
        ),
        cost_estimate=pl.CostEstimate(
            flops=9_000_000_000, bytes_accessed=20_000_000, transcendentals=17_000_000
        ),
    )(queries, pairs, pairs)


def pad_lanes(values):
    return jnp.pad(values, ((0, 0), (0, LANES - values.shape[1])))


def on_device(
    hidden_in,
    norm_gain,
    w_z,
    w_x,
    w_b,
    w_c,
    w_dt,
    conv_x,
    conv_b,
    conv_c,
    dt_bias,
    a_rate,
    skip_gain,
    group_gain,
    w_out,
    attn_gain,
    w_q,
    w_k,
    w_v,
):
    proj = gather_dot(
        hidden_in,
        norm_gain[None, :],
        jnp.concatenate([w_x, w_b, w_c, pad_lanes(w_dt), w_z], axis=1),
    )
    proj, w_out = lax.optimization_barrier((proj, w_out))
    out_columns = lax.all_gather(w_out, "seq", axis=1, tiled=True)
    heads = dt_bias.shape[0]
    groups = conv_b.shape[1] // N
    width = conv_x.shape[1] + conv_b.shape[1] + conv_c.shape[1]
    rim = from_behind(proj[proj.shape[0] - 8 :, :width], "seq", 1)
    y_normed = mixer(
        proj,
        rim,
        jnp.concatenate([conv_x, conv_b, conv_c], axis=1),
        pad_lanes(dt_bias[None, :]),
        pad_lanes(a_rate[None, :]),
        jnp.repeat(skip_gain, P_SIZE)[None, :],
        group_gain[None, :],
        heads,
        groups,
    )
    mixed, normed_two = output_stage(y_normed, out_columns, hidden_in, attn_gain[None, :])
    own_keys = jnp.dot(normed_two, w_k, preferred_element_type=F32).astype(BF16)
    own_values = jnp.dot(normed_two, w_v, preferred_element_type=F32).astype(BF16)
    pairs = lax.all_gather(
        jnp.concatenate([own_keys, own_values], axis=1), "seq", axis=0, tiled=True
    )
    queries = jnp.dot(normed_two, w_q, preferred_element_type=F32).astype(BF16)
    context = attention(queries, pairs, own_keys.shape[1] // HD)
    return (mixed, context)


def solution(mesh):
    placed = (
        P("seq", "mp"),
        P(),
        P("seq", "mp"),
        P("seq", "mp"),
        P("seq", "mp"),
        P("seq", "mp"),
        P("seq", "mp"),
        P(None, "mp"),
        P(None, "mp"),
        P(None, "mp"),
        P("mp"),
        P("mp"),
        P("mp"),
        P("mp"),
        P("mp", "seq"),
        P(),
        P(None, "mp"),
        P(None, "mp"),
        P(None, "mp"),
    )
    return jax.shard_map(
        on_device,
        mesh=mesh,
        in_specs=placed,
        out_specs=(P("seq", "mp"), P("seq", "mp")),
        check_vma=False,
    )
```

profile of v0, /device:TPU:25, one launch (start us, length us, event | category | flops | bytes accessed | tf_op | source)
XLA Modules:
  0.0 735.6 jit_solution(14783138053554212251)
XLA Ops:
  7.2 0.0 copy-start.7
  7.2 0.0 copy-start.5
  7.2 0.0 copy-start.6
  7.2 0.0 copy-start.3
  7.2 0.0 all-gather.3.cloned.1.call-start
  7.3 3.4 constant_dynamic-update-slice_fusion.3
  10.6 0.0 copy-done.7
  10.6 0.1 copy.21
  10.7 0.0 copy-done.5
  10.8 0.8 constant_dynamic-update-slice_fusion.2
  11.5 0.0 copy-done.6
  11.5 0.7 constant_dynamic-update-slice_fusion.1
  12.3 0.7 pad_dynamic-update-slice_fusion
  13.0 0.0 copy-done.3
  13.0 1.5 constant_dynamic-update-slice_fusion.w_ref
  14.5 0.0 copy-start.14
  14.5 0.0 copy-start.15
  14.5 0.0 copy-start.1
  14.5 330.2 %shard_map.194.proj_ref = f32[512,4736]{1,0:T(8,128)} custom-call(bf16[512,1024]{1,0:T(8,128)(2,1)} %hidden_ref.3, f32[1,4096]{1,0:T(1,128)} %bitcast.12, bf16[512,4736]{1,0:T(8,128)(2,1)} %constant_dynamic-update-slice_fusion.w_ref), custom_call_target="tpu_custom_call" | custom-call | flops 19864223744 | bytes 160000000 | tf_op jit(solution)/shard_map/pallas_call | solution.py:219
  344.7 0.0 all-gather.3.cloned.1.call-update
  344.7 0.0 all-gather.5.cloned.1.call-start
  344.8 0.9 slice.3
  345.7 1.3 collective-permute-start
  347.0 0.1 fusion.expand_ref
  347.1 0.0 copy-done.8
  347.1 0.0 copy-done.9
  347.1 0.0 copy-done.10
  347.1 0.1 broadcast_in_dim.23
  347.2 0.1 broadcast_in_dim_reshape.3.skip_ref
  347.3 1.5 collective-permute-done.rim_ref
  348.8 0.0 copy-done.1
  348.8 77.4 %shard_map.195.y_ref = bf16[512,2048]{1,0:T(8,128)(2,1)S(1)} custom-call(f32[512,4736]{1,0:T(8,128)} %shard_map.194.proj_ref, f32[8,2560]{1,0:T(8,128)S(1)} %collective-permute-done.rim_ref, f32[4,2560]{1,0:T(4,128)S(1)} %pad_maximum_fusion.1.taps_ref, f32[1,128]{1,0:T(1,128)S(1)} %pad.12.bias_ref, f32[1,128]{1,0:T(1,128)S(1)} %pad.13.rate_ref, ...), custom_call_target="tpu_custom_call" | custom-call | flops 8000000000 | bytes 100000000 | tf_op jit(solution)/shard_map/pallas_call | solution.py:439
  426.2 0.0 copy-start.2
  426.3 1.3 copy-done.2
  427.6 71.7 %all-gather.3.cloned.1.call-done.w_ref = bf16[2048,4096]{1,0:T(8,128)(2,1)} async-done(((bf16[2048,512]{1,0:T(8,128)(2,1)}), bf16[2048,4096]{1,0:T(8,128)(2,1)}) %all-gather.3.cloned.1.call-update) | async-done | bytes 16777232 | tf_op jit(solution)/shard_map/all_gather | solution.py:684
  499.3 110.3 %shard_map.196 = (f32[512,1024]{1,0:T(8,128)}, bf16[512,4096]{1,0:T(8,128)(2,1)}) custom-call(bf16[512,2048]{1,0:T(8,128)(2,1)} %copy-done.2, bf16[2048,4096]{1,0:T(8,128)(2,1)} %all-gather.3.cloned.1.call-done.w_ref, bf16[512,1024]{1,0:T(8,128)(2,1)} %hidden_ref.3, f32[1,4096]{1,0:T(1,128)} %bitcast.13), custom_call_target="tpu_custom_call" | custom-call | flops 8589934592 | bytes 60000000 | tf_op jit(solution)/shard_map/pallas_call | solution.py:542
  609.6 0.0 copy-start.13
  609.6 3.6 convolution_convert_fusion.1
  613.2 0.5 copy-done.16
  613.7 1.2 convolution_convert_fusion.2
  614.9 0.8 pad_maximum_fusion
  615.8 0.0 all-gather.5.cloned.1.call-update
  615.8 9.1 %convolution_convert_fusion.q_ref = bf16[512,1024]{1,0:T(8,128)(2,1)S(1)} fusion(bf16[512,4096]{1,0:T(8,128)(2,1)} %get-tuple-element.9, bf16[4096,1024]{1,0:T(8,128)(2,1)} %param.35), kind=kOutput, calls=%fused_computation | convolution fusion | flops 4295491584 | bytes 13631488 | tf_op jit(solution)/shard_map/dot_general | solution.py:706
  625.0 37.3 %all-gather.5.cloned.1.call-done.k_ref.v_ref = bf16[4096,512]{1,0:T(8,128)(2,1)} async-done(((bf16[512,512]{1,0:T(8,128)(2,1)}), bf16[4096,512]{1,0:T(8,128)(2,1)}) %all-gather.5.cloned.1.call-update) | async-done | bytes 4194320 | tf_op jit(solution)/shard_map/all_gather | solution.py:703
  662.2 2.2 copy-done
  664.4 63.0 %shard_map.197 = f32[512,1024]{1,0:T(8,128)} custom-call(bf16[512,1024]{1,0:T(8,128)(2,1)S(1)} %convolution_convert_fusion.q_ref, bf16[4096,512]{1,0:T(8,128)(2,1)S(1)} %copy-done, bf16[4096,512]{1,0:T(8,128)(2,1)S(1)} %copy-done), custom_call_target="tpu_custom_call" | custom-call | flops 8999999488 | bytes 20000000 | tf_op jit(solution)/shard_map/pallas_call | solution.py:629
  727.5 0.0 copy-done.4
  727.5 1.3 copy.31
  (17 shorter events, 0.1 us)
Async XLA Ops:
  7.2 3.5 copy-start.7
  7.2 3.6 copy-start.5
  7.2 4.4 copy-start.6
  7.2 5.8 copy-start.3
  7.2 492.1 %all-gather.3.cloned.1.call-start = ((), (), s32[]{:S(2)}) async-start(), calls=%async_computation | async-start | bytes 18874368 | tf_op jit(solution)/shard_map/all_gather | solution.py:684
  14.5 332.6 %copy-start.8 = (f32[4,2048]{1,0:T(4,128)S(1)}, f32[4,2048]{1,0:T(4,128)}, u32[]{:S(2)}) copy-start(f32[4,2048]{1,0:T(4,128)} %param.26) | copy-start | bytes 98308
  14.5 332.6 %copy-start.9 = (f32[4,256]{1,0:T(4,128)S(1)}, f32[4,256]{1,0:T(4,128)}, u32[]{:S(2)}) copy-start(f32[4,256]{1,0:T(4,128)} %param.28) | copy-start | bytes 12292
  14.5 332.6 %copy-start.10 = (f32[4,256]{1,0:T(4,128)S(1)}, f32[4,256]{1,0:T(4,128)}, u32[]{:S(2)}) copy-start(f32[4,256]{1,0:T(4,128)} %param.27) | copy-start | bytes 12292
  14.5 332.6 %copy-start.11 = (f32[32]{0:T(128)S(1)}, f32[32]{0:T(128)}, u32[]{:S(2)}) copy-start(f32[32]{0:T(128)} %param.31) | copy-start | bytes 388
  14.5 332.8 %copy-start.14 = (f32[32]{0:T(128)S(1)}, f32[32]{0:T(128)}, u32[]{:S(2)}) copy-start(f32[32]{0:T(128)} %param.29) | copy-start | bytes 388
  14.5 332.8 %copy-start.15 = (f32[32]{0:T(128)S(1)}, f32[32]{0:T(128)}, u32[]{:S(2)}) copy-start(f32[32]{0:T(128)} %param.30) | copy-start | bytes 388
  14.5 334.3 %copy-start.1 = (f32[2048]{0:T(1024)S(1)}, f32[2048]{0:T(1024)}, u32[]{:S(2)}) copy-start(f32[2048]{0:T(1024)} %param.32) | copy-start | bytes 24580
  344.7 317.5 %all-gather.5.cloned.1.call-start = ((), (), s32[]{:S(2)}) async-start(), calls=%async_computation.1 | async-start | bytes 4718592 | tf_op jit(solution)/shard_map/all_gather | solution.py:703
  345.7 3.2 collective-permute-start
  426.2 1.3 copy-start.2
  499.3 110.3 %copy-start.12 = (bf16[4096,256]{1,0:T(8,128)(2,1)S(1)}, bf16[4096,256]{1,0:T(8,128)(2,1)}, u32[]{:S(2)}) copy-start(bf16[4096,256]{1,0:T(8,128)(2,1)} %param.37) | copy-start | bytes 6291460
  609.6 3.6 copy-start.13
  609.6 4.1 copy-start.16
  662.2 2.2 copy-start
  664.4 63.0 %copy-start.4 = (f32[512,1024]{1,0:T(8,128)S(1)}, f32[512,1024]{1,0:T(8,128)}, u32[]{:S(2)}) copy-start(f32[512,1024]{1,0:T(8,128)} %get-tuple-element.12) | copy-start | bytes 6291460
Sparse Core Ops, SparseCore 0:
  344.9 154.3 all-gather.2
  615.9 46.2 all-gather.4
where the time goes:
time: 736 us
  Pallas kernels  581 us (79%)
  waiting for transfers between devices  111 us (15%)
  between operations  14.3 us (2%)
  matrix products  14 us (2%)
  local copies, waits for them, and re-layouts  13.6 us (2%)
    pallas_call x1, Pallas kernels, gather_dot(): pl.pallas_call(functools.partial(gather_dot_kernel, n, m), out_shape=jax....  330 us
    pallas_call x1, Pallas kernels, output_stage(): pl.pallas_call(functools.partial(output_kernel, m), out_shape=(jax.ShapeD...  110 us
    pallas_call x1, Pallas kernels, mixer(): pl.pallas_call(functools.partial(mixer_kernel, n, heads, groups), out_sha...  77.4 us
    all_gather x1, waiting for transfers between devices, on_device(): out_columns = lax.all_gather(w_out, 'seq', axis=1, tiled=True)  71.7 us
    pallas_call x1, Pallas kernels, attention(): pl.pallas_call(functools.partial(attention_kernel, n, rows), grid=(kv_hea...  63 us
    all_gather x1, waiting for transfers between devices, on_device(): lax.all_gather(jnp.concatenate([own_keys, own_values], axis=1), 'seq', ax...  37.3 us
  transfers between devices with their start and end apart: 3, of which 3 were waited for; matrix products, arithmetic and copies ran while one was open for 1% of the time, Pallas kernels for 11%

commit v1 on v0

--- a/solution.py
+++ b/solution.py
@@ -654,6 +654,571 @@
     return jnp.pad(values, ((0, 0), (0, LANES - values.shape[1])))
 
 
+def spread_kernel(
+    n,
+    groups,
+    hidden_ref,
+    gain_ref,
+    wx_ref,
+    wz_ref,
+    wbc_ref,
+    wdt_ref,
+    all_ref,
+    w_ref,
+    dt_ref,
+    own,
+    cols,
+    sums,
+    local_sem,
+    send_sem,
+    recv_sem,
+):
+    me = lax.axis_index("seq")
+    member = lax.axis_index("mp")
+    chips = n // 2
+    z, c = me // 2, lax.rem(me, 2)
+    partner = 2 * z + 1 - c
+    across = member + 1 - 2 * lax.rem(member, 2)
+    along = lax.rem(member + 2, 4)
+    far = 3 - member
+    rows, wide = own.shape
+    depth = wx_ref.shape[0]
+    piece = wx_ref.shape[1] // n
+    pair = wbc_ref.shape[1] // groups
+
+    names, started = {}, []
+
+    def sem_of(key):
+        return recv_sem.at[names.setdefault(key, len(names))]
+
+    def guarded(cond, body):
+        if cond is True:
+            body()
+        else:
+            pl.when(cond)(body)
+
+    def send(cond, make_refs, key, **target):
+        index = len(started)
+
+        def make():
+            source, place = make_refs()
+            return pltpu.make_async_remote_copy(
+                src_ref=source,
+                dst_ref=place,
+                send_sem=send_sem.at[index],
+                recv_sem=sem_of(key),
+                device_id=target,
+                device_id_type=pl.DeviceIdType.MESH,
+            )
+
+        started.append((cond, make))
+        guarded(cond, lambda: make().start())
+
+    def arrived(cond, make_ref, key):
+        def body():
+            place = make_ref()
+            pltpu.make_async_copy(place, place, sem_of(key)).wait()
+
+        guarded(cond, body)
+
+    def both(first, second):
+        return second if first is True else jnp.logical_and(first, second)
+
+    barrier = pltpu.get_barrier_semaphore()
+    for d in range(1, n):
+        signal_seq(barrier, lax.rem(me + d, n))
+    for other in (across, along, far):
+        signal_mp(barrier, other)
+    pl.semaphore_wait(barrier, n - 1 + 3)
+
+    def rows_of(chip, core):
+        return pl.ds(pl.multiple_of((2 * chip + core) * depth, depth), depth)
+
+    def send_weights(way, d, same, cond, chip):
+        core = c if same else 1 - c
+        target = 2 * chip + core
+        here = pl.ds(pl.multiple_of(me * depth, depth), depth)
+        take = pl.ds(pl.multiple_of(target * piece, piece), piece)
+        group = target * groups // n
+        key = ("w", way, d, same)
+        send(cond, lambda: (wx_ref.at[:, take], w_ref.at[here, 0:piece]), key, seq=target)
+        send(cond, lambda: (wz_ref.at[:, take], w_ref.at[here, piece : 2 * piece]), key, seq=target)
+        if same or d == 0:
+            send(
+                cond,
+                lambda: (
+                    wbc_ref.at[:, pl.ds(pl.multiple_of(group * pair, pair), pair)],
+                    w_ref.at[here, 2 * piece : 2 * piece + pair],
+                ),
+                key,
+                seq=target,
+            )
+        send(cond, lambda: (wdt_ref, dt_ref.at[:, here]), ("dt", way, d, same), seq=target)
+
+    def weights_at(d):
+        for way in (1, -1):
+            chip = z + way * d
+            cond = chip <= chips - 1 if way == 1 else chip >= 0
+            for same in (True, False):
+                send_weights(way, d, same, cond, chip)
+
+    send_weights(0, 0, False, True, z)
+    here = pl.ds(pl.multiple_of(me * depth, depth), depth)
+    take = pl.ds(pl.multiple_of(me * piece, piece), piece)
+    group = pl.ds(pl.multiple_of(me * groups // n * pair, pair), pair)
+    locals_ = [
+        pltpu.make_async_copy(wx_ref.at[:, take], w_ref.at[here, 0:piece], local_sem.at[0]),
+        pltpu.make_async_copy(wz_ref.at[:, take], w_ref.at[here, piece : 2 * piece], local_sem.at[1]),
+        pltpu.make_async_copy(
+            wbc_ref.at[:, group], w_ref.at[here, 2 * piece : 2 * piece + pair], local_sem.at[2]
+        ),
+        pltpu.make_async_copy(wdt_ref, dt_ref.at[:, here], local_sem.at[3]),
+    ]
+    for copy in locals_:
+        copy.start()
+
+    tile = min(64, rows)
+
+    def square(i, carry):
+        at = pl.ds(pl.multiple_of(i * tile, tile), tile)
+        v = hidden_ref[at, :].astype(F32)
+        cols[at, :] = jnp.broadcast_to(jnp.sum(v * v, axis=-1, keepdims=True), (tile, LANES))
+        return carry
+
+    lax.fori_loop(0, rows // tile, square, 0)
+    sums[0] = jnp.transpose(cols[...])[0:8, :]
+    for i, other in enumerate((across, along, far)):
+        send(True, lambda i=i: (sums.at[0], sums.at[i + 1]), ("sum", i), mp=other)
+    for i in range(3):
+        arrived(True, lambda i=i: sums.at[i + 1], ("sum", i))
+    power = sums[0] + sums[1] + sums[2] + sums[3]
+    cols[...] = jnp.transpose(jnp.broadcast_to(power[0:1, :], (LANES, rows)))
+
+    def normalise(i, carry):
+        at = pl.ds(pl.multiple_of(i * tile, tile), tile)
+        scale = lax.rsqrt(cols[at, 0:1] / (4 * wide) + 1e-05)
+        own[at, :] = (hidden_ref[at, :].astype(F32) * scale * gain_ref[...]).astype(BF16)
+        return carry
+
+    lax.fori_loop(0, rows // tile, normalise, 0)
+
+    def valid(slot):
+        kind, d = slot
+        return True if d == 0 else z >= d if kind == "b" else z + d <= chips - 1
+
+    def region(slot, owner, half=None, core=None):
+        kind, d = slot
+        origin = z - d if kind == "b" else z + d
+        core = c if core is None else core
+        start = (2 * origin + core) * rows
+        size = rows
+        if half is not None:
+            size = rows // 2
+            start = start + half * size
+        return all_ref.at[
+            pl.ds(pl.multiple_of(start, size), size),
+            pl.ds(pl.multiple_of(owner * wide, wide), wide),
+        ]
+
+    def stage_a(slot):
+        kind, d = slot
+        ok = valid(slot)
+        if d:
+            arrived(ok, lambda: region(slot, member), ("col", slot))
+
+        def source():
+            return region(slot, member) if d else own
+
+        if d < chips - 1:
+            if kind in "ob":
+                up = both(ok, z + 1 <= chips - 1)
+                send(up, lambda: (source(), region(slot, member)), ("col", ("b", d + 1)), seq=me + 2)
+            if kind in "oa":
+                down = both(ok, z >= 1)
+                send(down, lambda: (source(), region(slot, member)), ("col", ("a", d + 1)), seq=me - 2)
+        send(ok, lambda: (source(), region(slot, member)), ("px", slot), mp=across)
+        send(ok, lambda: (source(), region(slot, member)), ("py", slot), mp=along)
+        send(ok, lambda: (source(), region(slot, member)), ("d", "col", slot), seq=partner)
+
+    def stage_b(slot):
+        ok = valid(slot)
+        for q, owner, half, nxt in (("px", across, 0, along), ("py", along, 1, across)):
+            arrived(ok, lambda: region(slot, owner), (q, slot))
+            send(
+                ok,
+                lambda owner=owner, half=half: (region(slot, owner, half), region(slot, owner, half)),
+                ("half", half, slot),
+                mp=nxt,
+            )
+            send(
+                ok,
+                lambda owner=owner: (region(slot, owner), region(slot, owner)),
+                ("d", q, slot),
+                seq=partner,
+            )
+
+    def stage_c(slot):
+        ok = valid(slot)
+        for half in range(2):
+            arrived(ok, lambda: region(slot, far, half), ("half", half, slot))
+        send(ok, lambda: (region(slot, far), region(slot, far)), ("d", "far", slot), seq=partner)
+
+    own_copy = pltpu.make_async_copy(own, region(("o", 0), member), local_sem.at[4])
+    own_copy.start()
+    locals_.append(own_copy)
+
+    def step(stage, d):
+        for slot in ((("o", 0),) if d == 0 else (("b", d), ("a", d))):
+            stage(slot)
+
+    last = chips - 1
+    for t in range(chips + 2):
+        if t <= last:
+            step(stage_a, t)
+            if last - t >= 1:
+                weights_at(last - t)
+        if 0 <= t - 1 <= last:
+            step(stage_b, t - 1)
+        if 0 <= t - 2 <= last:
+            step(stage_c, t - 2)
+
+    ways = [(way, d) for d in range(1, chips) for way in (1, -1)]
+
+    def origin_of(way, d):
+        chip = z - way * d
+        return chip, (chip >= 0 if way == 1 else chip <= chips - 1)
+
+    for way, d in ways:
+        chip, ok = origin_of(way, d)
+        arrived(ok, lambda: w_ref.at[rows_of(chip, c), :], ("w", way, d, True))
+
+        def shared(chip=chip):
+            place = w_ref.at[rows_of(chip, c), 2 * piece : 2 * piece + pair]
+            return place, place
+
+        send(ok, shared, ("wd", way, d), seq=partner)
+    for way, d in ways:
+        chip, ok = origin_of(way, d)
+        arrived(ok, lambda: w_ref.at[rows_of(chip, 1 - c), 0 : 2 * piece], ("w", way, d, False))
+        arrived(
+            ok,
+            lambda: w_ref.at[rows_of(chip, 1 - c), 2 * piece : 2 * piece + pair],
+            ("wd", way, d),
+        )
+        for same in (True, False):
+            core = c if same else 1 - c
+            arrived(ok, lambda: dt_ref.at[:, rows_of(chip, core)], ("dt", way, d, same))
+    arrived(True, lambda: w_ref.at[rows_of(z, 1 - c), :], ("w", 0, 0, False))
+    arrived(True, lambda: dt_ref.at[:, rows_of(z, 1 - c)], ("dt", 0, 0, False))
+    for d in range(chips):
+        for slot in ((("o", 0),) if d == 0 else (("b", d), ("a", d))):
+            for q, owner in (("col", member), ("px", across), ("py", along), ("far", far)):
+                arrived(valid(slot), lambda: region(slot, owner, None, 1 - c), ("d", q, slot))
+    for copy in locals_:
+        copy.wait()
+    for cond, make in started:
+        guarded(cond, lambda: make().wait_send())
+
+
+def spread(hidden, gain, w_x, w_z, w_bc, w_dt, groups):
+    n = lax.axis_size("seq")
+    rows, wide = hidden.shape
+    depth = w_x.shape[0]
+    cols = 2 * (w_x.shape[1] // n) + w_bc.shape[1] // groups
+    anywhere = pl.BlockSpec(memory_space=pl.ANY)
+    vmem = pl.BlockSpec(memory_space=pltpu.VMEM)
+    return pl.pallas_call(
+        functools.partial(spread_kernel, n, groups),
+        out_shape=(
+            jax.ShapeDtypeStruct((n * rows, 4 * wide), BF16),
+            jax.ShapeDtypeStruct((n * depth, cols), BF16),
+            jax.ShapeDtypeStruct((w_dt.shape[0], n * depth), BF16),
+        ),
+        in_specs=[vmem, vmem] + [anywhere] * 4,
+        out_specs=(anywhere,) * 3,
+        scratch_shapes=[
+            pltpu.VMEM((rows, wide), BF16),
+            pltpu.VMEM((rows, LANES), F32),
+            pltpu.VMEM((4, 8, rows), F32),
+            pltpu.SemaphoreType.DMA((5,)),
+            pltpu.SemaphoreType.DMA((45 * n // 2,)),
+            pltpu.SemaphoreType.DMA((30 * n // 2,)),
+        ],
+        compiler_params=pltpu.CompilerParams(
+            collective_id=3, has_side_effects=True, vmem_limit_bytes=24 * 1024 * 1024
+        ),
+        cost_estimate=pl.CostEstimate(
+            flops=20_000_000_000, bytes_accessed=100_000_000, transcendentals=0
+        ),
+    )(hidden, gain, w_x, w_z, w_bc, w_dt)
+
+
+def heads_kernel(
+    n,
+    groups,
+    hidden_ref,
+    w_ref,
+    wdt_ref,
+    taps_ref,
+    bias_ref,
+    rate_ref,
+    skip_ref,
+    gain_ref,
+    y_ref,
+    blocks,
+    wdt_own,
+    window,
+    gate,
+    raws,
+    conv,
+    state,
+    out,
+    landed,
+    load_sem,
+    send_sem,
+    recv_sem,
+):
+    me = lax.axis_index("seq")
+    rows = blocks.shape[1]
+    inner = gate.shape[1]
+    width = inner + 2 * N
+    heads = inner // P_SIZE
+    kw = taps_ref.shape[0]
+
+    barrier = pltpu.get_barrier_semaphore()
+    for d in range(1, n):
+        signal_seq(barrier, lax.rem(me + d, n))
+    pl.semaphore_wait(barrier, n - 1)
+
+    def load(i, slot):
+        return pltpu.make_async_copy(
+            hidden_ref.at[pl.ds(pl.multiple_of(i * rows, rows), rows), :],
+            blocks.at[slot],
+            load_sem.at[slot],
+        )
+
+    load(0, 0).start()
+    all_heads = wdt_ref.shape[0]
+    pick_row = lax.broadcasted_iota(jnp.int32, (LANES, all_heads), 0)
+    pick_col = lax.broadcasted_iota(jnp.int32, (LANES, all_heads), 1)
+    chosen = jnp.logical_and(pick_col == me * heads + pick_row, pick_row < heads)
+    wdt_own[...] = jnp.dot(
+        jnp.where(chosen, 1.0, 0.0).astype(BF16), wdt_ref[...], preferred_element_type=F32
+    ).astype(BF16)
+
+    lane_head = lax.broadcasted_iota(jnp.int32, (LANES, inner), 1) // P_SIZE
+    expand = jnp.where(
+        lax.broadcasted_iota(jnp.int32, (LANES, inner), 0) == lane_head, 1.0, 0.0
+    ).astype(BF16)
+    window[0:8, :] = jnp.zeros((8, width), F32)
+    state[...] = jnp.zeros_like(state)
+    row_id = lax.broadcasted_iota(jnp.int32, (QB, QB), 0)
+    col_id = lax.broadcasted_iota(jnp.int32, (QB, QB), 1)
+    causal = row_id >= col_id
+    low_lanes = col_id < P_SIZE
+    tri = jnp.where(causal, 1.0, 0.0).astype(F32)
+
+    def hand_over(i):
+        return pltpu.make_async_remote_copy(
+            src_ref=out.at[i],
+            dst_ref=landed.at[me],
+            send_sem=send_sem.at[i],
+            recv_sem=recv_sem.at[me],
+            device_id={"seq": i},
+            device_id_type=pl.DeviceIdType.MESH,
+        )
+
+    def block(i, carry_none):
+        slot = lax.rem(i, 2)
+
+        @pl.when(i + 1 < n)
+        def _():
+            load(i + 1, 1 - slot).start()
+
+        load(i, slot).wait()
+        source = blocks.at[slot]
+        window[8 : 8 + rows, 0:inner] = jnp.dot(
+            source[...], w_ref[:, 0:inner], preferred_element_type=F32
+        )
+        gate[...] = jnp.dot(source[...], w_ref[:, inner : 2 * inner], preferred_element_type=F32)
+        window[8 : 8 + rows, inner:width] = jnp.dot(
+            source[...], w_ref[:, 2 * inner : 2 * inner + 2 * N], preferred_element_type=F32
+        )
+        raws[...] = lax.dot_general(
+            source[...], wdt_own[...], (((1,), (1,)), ((), ())), preferred_element_type=F32
+        )
+        for sub in range(rows // QB):
+            at = sub * QB
+            here = slice(at, at + QB)
+            for start in range(0, width, LANES):
+                cs = slice(start, start + LANES)
+                total = None
+                for j in range(kw):
+                    first = 8 - kw + 1 + j + at
+                    term = taps_ref[j : j + 1, cs] * window[first : first + QB, cs]
+                    total = term if total is None else total + term
+                conv[sub, :, cs] = silu(total)
+            raw = raws[here, :] + bias_ref[...]
+            steps = jnp.maximum(raw, 0.0) + jnp.log1p(jnp.exp(-jnp.abs(raw)))
+            decays = -rate_ref[...] * steps
+            cum = jnp.dot(tri, decays, precision=HIGH, preferred_element_type=F32)
+            cum_t = jnp.transpose(cum)
+            grown = jnp.exp(cum)
+            tail = jnp.exp(cum[QB - 1 : QB, :] - cum)
+            x = conv[sub, :, 0:inner]
+            b = conv[sub, :, inner : inner + N].astype(BF16)
+            c = conv[sub, :, inner + N : width].astype(BF16)
+            scaled = x * spread_heads(steps, expand)
+            grown_e = spread_heads(grown, expand)
+            tailed = (scaled * spread_heads(tail, expand)).astype(BF16)
+            scaled_low = scaled.astype(BF16)
+            held = state[...]
+            carried = grown_e * jnp.dot(c, held.astype(BF16), preferred_element_type=F32)
+            fresh = lax.dot_general(b, tailed, (((0,), (0,)), ((), ())), preferred_element_type=F32)
+            state[...] = grown_e[QB - 1 : QB, :] * held + fresh
+            affinity = lax.dot_general(c, b, (((1,), (1,)), ((), ())), preferred_element_type=F32)
+            affinity = jnp.where(causal, affinity, 0.0)
+            full = carried + skip_ref[...] * x
+            for pair in range(inner // LANES):
+                lanes = slice(pair * LANES, (pair + 1) * LANES)
+                outs = []
+                for k in range(2):
+                    h = pair * 2 + k
+                    spread_h = jnp.minimum(cum[:, h : h + 1] - cum_t[h : h + 1, :], 0.0)
+                    mixing = (affinity * jnp.exp(spread_h)).astype(BF16)
+                    outs.append(
+                        jnp.dot(mixing, scaled_low[:, lanes], preferred_element_type=F32)
+                    )
+                inside = jnp.where(low_lanes, outs[0], outs[1])
+                out[i, here, lanes] = (
+                    (full[:, lanes] + inside) * silu(gate[here, lanes])
+                ).astype(BF16)
+        window[0:8, :] = window[rows : rows + 8, :]
+
+        @pl.when(i != me)
+        def _():
+            hand_over(i).start()
+
+        return carry_none
+
+    lax.fori_loop(0, n, block, 0)
+
+    for s in range(n):
+
+        @pl.when(s != me)
+        def _():
+            pltpu.make_async_copy(landed.at[s], landed.at[s], recv_sem.at[s]).wait()
+
+        @pl.when(s == me)
+        def _():
+            landed[s] = out[s]
+
+    per = n // groups
+    for g in range(groups):
+        members = range(g * per, (g + 1) * per)
+
+        def finish(i, carry_none):
+            at = pl.ds(pl.multiple_of(i * QB, QB), QB)
+            power = None
+            for s in members:
+                v = landed[s, at, :].astype(F32)
+                part = jnp.sum(v * v, axis=-1, keepdims=True)
+                power = part if power is None else power + part
+            scale = lax.rsqrt(power / (per * inner) + 1e-05)
+            for s in members:
+                lanes = slice(s * inner, (s + 1) * inner)
+                v = landed[s, at, :].astype(F32)
+                y_ref[at, lanes] = (v * scale * gain_ref[:, lanes]).astype(BF16)
+            return carry_none
+
+        lax.fori_loop(0, rows // QB, finish, 0)
+    for s in range(n):
+
+        @pl.when(s != me)
+        def _():
+            hand_over(s).wait_send()
+
+
+def mix_heads(hidden, weights, w_dt, taps, bias, rate, skip, gain, groups):
+    n = lax.axis_size("seq")
+    rows = hidden.shape[0] // n
+    features = hidden.shape[1]
+    inner = skip.shape[1]
+    width = inner + 2 * N
+    vmem = pl.BlockSpec(memory_space=pltpu.VMEM)
+    return pl.pallas_call(
+        functools.partial(heads_kernel, n, groups),
+        out_shape=jax.ShapeDtypeStruct((rows, n * inner), BF16),
+        in_specs=[pl.BlockSpec(memory_space=pl.ANY)] + [vmem] * 7,
+        out_specs=vmem,
+        scratch_shapes=[
+            pltpu.VMEM((2, rows, features), BF16),
+            pltpu.VMEM((LANES, features), BF16),
+            pltpu.VMEM((8 + rows, width), F32),
+            pltpu.VMEM((rows, inner), F32),
+            pltpu.VMEM((rows, LANES), F32),
+            pltpu.VMEM((rows // QB, QB, width), F32),
+            pltpu.VMEM((N, inner), F32),
+            pltpu.VMEM((n, rows, inner), BF16),
+            pltpu.VMEM((n, rows, inner), BF16),
+            pltpu.SemaphoreType.DMA((2,)),
+            pltpu.SemaphoreType.DMA((n,)),
+            pltpu.SemaphoreType.DMA((n,)),
+        ],
+        compiler_params=pltpu.CompilerParams(
+            collective_id=4, has_side_effects=True, vmem_limit_bytes=48 * 1024 * 1024
+        ),
+        cost_estimate=pl.CostEstimate(
+            flops=40_000_000_000, bytes_accessed=50_000_000, transcendentals=8_000_000
+        ),
+    )(hidden, weights, w_dt, taps, bias, rate, skip, gain)
+
+
+def own_slice(values, index, size):
+    return lax.dynamic_slice_in_dim(values, index * size, size, values.ndim - 1)
+
+
+def mixer_by_heads(
+    hidden_in, norm_gain, w_z, w_x, w_b, w_c, w_dt, conv_x, conv_b, conv_c, dt_bias, a_rate,
+    skip_gain, group_gain,
+):
+    n = lax.axis_size("seq")
+    me = lax.axis_index("seq")
+    groups = conv_b.shape[1] // N
+    inner = conv_x.shape[1] // n
+    heads = dt_bias.shape[0] // n
+    group = me * groups // n
+    pieces = []
+    for g in range(groups):
+        pieces += [w_b[:, g * N : (g + 1) * N], w_c[:, g * N : (g + 1) * N]]
+    gain = own_slice(norm_gain[None, :], lax.axis_index("mp"), hidden_in.shape[1])
+    hidden, weights, steps = spread(
+        hidden_in, gain, w_x, w_z, jnp.concatenate(pieces, axis=1), jnp.transpose(w_dt), groups
+    )
+    taps = jnp.concatenate(
+        [own_slice(conv_x, me, inner), own_slice(conv_b, group, N), own_slice(conv_c, group, N)],
+        axis=1,
+    )
+    return hidden, functools.partial(
+        mix_heads,
+        weights=weights,
+        w_dt=steps,
+        taps=taps,
+        bias=pad_lanes(own_slice(dt_bias[None, :], me, heads)),
+        rate=pad_lanes(own_slice(a_rate[None, :], me, heads)),
+        skip=jnp.repeat(own_slice(skip_gain[None, :], me, heads), P_SIZE, axis=1),
+        gain=group_gain[None, :],
+        groups=groups,
+    )
+
+
+def splits_by_heads(conv_x, conv_b):
+    n, m = lax.axis_size("seq"), lax.axis_size("mp")
+    groups = conv_b.shape[1] // N
+    whole = conv_x.shape[1] % (n * LANES) == 0 and n % groups == 0
+    return m == 4 and n % 2 == 0 and n >= 4 and whole
+
+
 def on_device(
     hidden_in,
     norm_gain,
@@ -675,28 +1240,37 @@
     w_k,
     w_v,
 ):
-    proj = gather_dot(
-        hidden_in,
-        norm_gain[None, :],
-        jnp.concatenate([w_x, w_b, w_c, pad_lanes(w_dt), w_z], axis=1),
-    )
-    proj, w_out = lax.optimization_barrier((proj, w_out))
-    out_columns = lax.all_gather(w_out, "seq", axis=1, tiled=True)
-    heads = dt_bias.shape[0]
-    groups = conv_b.shape[1] // N
-    width = conv_x.shape[1] + conv_b.shape[1] + conv_c.shape[1]
-    rim = from_behind(proj[proj.shape[0] - 8 :, :width], "seq", 1)
-    y_normed = mixer(
-        proj,
-        rim,
-        jnp.concatenate([conv_x, conv_b, conv_c], axis=1),
-        pad_lanes(dt_bias[None, :]),
-        pad_lanes(a_rate[None, :]),
-        jnp.repeat(skip_gain, P_SIZE)[None, :],
-        group_gain[None, :],
-        heads,
-        groups,
-    )
+    if splits_by_heads(conv_x, conv_b):
+        hidden, mix = mixer_by_heads(
+            hidden_in, norm_gain, w_z, w_x, w_b, w_c, w_dt, conv_x, conv_b, conv_c, dt_bias,
+            a_rate, skip_gain, group_gain,
+        )
+        hidden, w_out = lax.optimization_barrier((hidden, w_out))
+        out_columns = lax.all_gather(w_out, "seq", axis=1, tiled=True)
+        y_normed = mix(hidden)
+    else:
+        proj = gather_dot(
+            hidden_in,
+            norm_gain[None, :],
+            jnp.concatenate([w_x, w_b, w_c, pad_lanes(w_dt), w_z], axis=1),
+        )
+        proj, w_out = lax.optimization_barrier((proj, w_out))
+        out_columns = lax.all_gather(w_out, "seq", axis=1, tiled=True)
+        heads = dt_bias.shape[0]
+        groups = conv_b.shape[1] // N
+        width = conv_x.shape[1] + conv_b.shape[1] + conv_c.shape[1]
+        rim = from_behind(proj[proj.shape[0] - 8 :, :width], "seq", 1)
+        y_normed = mixer(
+            proj,
+            rim,
+            jnp.concatenate([conv_x, conv_b, conv_c], axis=1),
+            pad_lanes(dt_bias[None, :]),
+            pad_lanes(a_rate[None, :]),
+            jnp.repeat(skip_gain, P_SIZE)[None, :],
+            group_gain[None, :],
+            heads,
+            groups,
+        )
     mixed, normed_two = output_stage(y_normed, out_columns, hidden_in, attn_gain[None, :])
     own_keys = jnp.dot(normed_two, w_k, preferred_element_type=F32).astype(BF16)
     own_values = jnp.dot(normed_two, w_v, preferred_element_type=F32).astype(BF16)

time: 736 us -> 666 us (0.905)
  waiting for transfers between devices: 111 us -> 74.6 us
  Pallas kernels: 581 us -> 546 us
    pallas_call x2, Pallas kernels: 408 us -> 373 us  [the longest x1 220 us: spread(): pl.pallas_call(functools.partial(spread_kernel, n, groups), out_shape=(ja...]
    all_gather x1, waiting for transfers between devices: 71.7 us -> 37.3 us  [on_device(): out_columns = lax.all_gather(w_out, 'seq', axis=1, tiled=True)]
  transfers between devices with their start and end apart: 3 -> 2, of which waited for: 3 -> 2; matrix products, arithmetic and copies ran while one was open for 1% -> 2% of each run, Pallas kernels for 11% -> 23%
where the time goes in v1:
time: 666 us; the launch traced here: 665 us
  Pallas kernels  546 us (82%)
  waiting for transfers between devices  74.6 us (11%)
  local copies, waits for them, and re-layouts  16 us (2%)
  between operations  14.2 us (2%)
  matrix products  14 us (2%)
    pallas_call x1, Pallas kernels, spread(): pl.pallas_call(functools.partial(spread_kernel, n, groups), out_shape=(ja...  220 us
    pallas_call x1, Pallas kernels, mix_heads(): pl.pallas_call(functools.partial(heads_kernel, n, groups), out_shape=jax....  153 us
    pallas_call x1, Pallas kernels, output_stage(): pl.pallas_call(functools.partial(output_kernel, m), out_shape=(jax.ShapeD...  110 us
    pallas_call x1, Pallas kernels, attention(): pl.pallas_call(functools.partial(attention_kernel, n, rows), grid=(kv_hea...  63 us
    all_gather x1, waiting for transfers between devices, on_device(): lax.all_gather(jnp.concatenate([own_keys, own_values], axis=1), 'seq', ax...  37.3 us
    all_gather x1, waiting for transfers between devices, on_device(): out_columns = lax.all_gather(w_out, 'seq', axis=1, tiled=True)  37.3 us
  transfers between devices with their start and end apart: 2, of which 2 were waited for; matrix products, arithmetic and copies ran while one was open for 2% of the time, Pallas kernels for 23%

profile of v1, /device:TPU:25, one launch (start us, length us, event | category | flops | bytes accessed | tf_op | source)
XLA Modules:
  0.0 665.5 jit_solution(17413743642750535070)
XLA Ops:
  7.2 0.0 copy-start
  7.2 0.0 all-gather.3.cloned.1.call-start
  7.2 0.8 dynamic-slice.12
  8.1 1.1 fusion
  9.2 0.1 pad_maximum_fusion.wbc_ref
  9.3 0.0 copy-start.2
  9.3 1.6 copy-done.2
  10.9 1.6 copy-done.3
  12.5 1.2 copy-done.4
  13.7 0.8 copy-done.5
  14.4 0.0 copy-start.11
  14.5 0.0 copy-start.6
  14.5 219.6 %shard_map.194 = (bf16[4096,4096]{1,0:T(8,128)(2,1)}, bf16[4096,768]{1,0:T(8,128)(2,1)S(1)}, bf16[32,4096]{1,0:T(8,128)(2,1)S(1)}) custom-call(bf16[512,1024]{1,0:T(8,128)(2,1)S(1)} %copy-done.4, f32[1,1024]{1,0:T(1,128)S(1)} %bitcast.14, bf16[512,2048]{1,0:T(8,128)(2,1)S(1)} %copy-done.2, bf16[512,2048]{1,0:T(8,128)(2,1)S(1)} %copy-done.3, ...), custom_call_target="tpu_custom_call" | custom-call | flops 20000000000 | bytes 100000000 | tf_op jit(solution)/shard_map/pallas_call | solution.py:930
  234.1 0.0 copy-start.8
  234.1 2.6 copy-done.8
  236.7 0.0 all-gather.3.cloned.1.call-update
  236.7 0.0 all-gather.5.cloned.1.call-start
  236.8 0.0 copy-done.15
  236.8 0.1 dynamic-slice.15
  236.9 0.0 copy-done.12
  236.9 0.0 copy-done.13
  236.9 0.1 dynamic-slice_bitcast_fusion
  237.0 0.1 broadcast_in_dim.15
  237.0 0.1 broadcast_in_dim.16.skip_ref
  237.1 0.7 constant_dynamic-slice_fusion.2
  237.8 0.0 copy-done.10
  237.8 0.0 copy-done.11
  237.8 0.0 copy-done.6
  237.8 153.1 %shard_map.195.y_ref = bf16[512,2048]{1,0:T(8,128)(2,1)S(1)} custom-call(bf16[4096,4096]{1,0:T(8,128)(2,1)} %get-tuple-element.10.hidden_ref, bf16[4096,768]{1,0:T(8,128)(2,1)} %copy-done.8, bf16[32,4096]{1,0:T(8,128)(2,1)S(1)} %get-tuple-element.12.wdt_ref, f32[4,512]{1,0:T(4,128)S(1)} %pad_maximum_fusion.2.taps_ref, f32[1,128]{1,0:T(1,128)S(1)} %pad.7.bias_ref, ...), custom_call_target="tpu_custom_call" | custom-call | flops 40000000000 | bytes 50000000 | tf_op jit(solution)/shard_map/pallas_call | solution.py:1149
  390.9 0.0 copy-start.7
  390.9 1.3 copy-done.7
  392.2 37.3 %all-gather.3.cloned.1.call-done.w_ref = bf16[2048,4096]{1,0:T(8,128)(2,1)} async-done(((bf16[2048,512]{1,0:T(8,128)(2,1)}), bf16[2048,4096]{1,0:T(8,128)(2,1)}) %all-gather.3.cloned.1.call-update) | async-done | bytes 16777232 | tf_op jit(solution)/shard_map/all_gather | solution.py:1249
  429.5 109.9 %shard_map.196 = (f32[512,1024]{1,0:T(8,128)}, bf16[512,4096]{1,0:T(8,128)(2,1)}) custom-call(bf16[512,2048]{1,0:T(8,128)(2,1)} %copy-done.7, bf16[2048,4096]{1,0:T(8,128)(2,1)} %all-gather.3.cloned.1.call-done.w_ref, bf16[512,1024]{1,0:T(8,128)(2,1)} %hidden_ref.3, f32[1,4096]{1,0:T(1,128)} %bitcast.17), custom_call_target="tpu_custom_call" | custom-call | flops 8589934592 | bytes 60000000 | tf_op jit(solution)/shard_map/pallas_call | solution.py:542
  539.4 0.0 copy-start.14
  539.5 0.0 copy-start.16
  539.5 0.0 copy-done
  539.5 3.6 convolution_convert_fusion.1
  543.1 0.0 copy-done.14
  543.1 0.5 copy-done.16
  543.5 1.2 convolution_convert_fusion.2
  544.8 0.8 pad_maximum_fusion.1
  545.6 0.0 all-gather.5.cloned.1.call-update
  545.6 9.1 %convolution_convert_fusion.q_ref = bf16[512,1024]{1,0:T(8,128)(2,1)S(1)} fusion(bf16[512,4096]{1,0:T(8,128)(2,1)} %get-tuple-element.15, bf16[4096,1024]{1,0:T(8,128)(2,1)} %param.35), kind=kOutput, calls=%fused_computation | convolution fusion | flops 4295491584 | bytes 13631488 | tf_op jit(solution)/shard_map/dot_general | solution.py:1280
  554.8 37.3 %all-gather.5.cloned.1.call-done.k_ref.v_ref = bf16[4096,512]{1,0:T(8,128)(2,1)} async-done(((bf16[512,512]{1,0:T(8,128)(2,1)}), bf16[4096,512]{1,0:T(8,128)(2,1)}) %all-gather.5.cloned.1.call-update) | async-done | bytes 4194320 | tf_op jit(solution)/shard_map/all_gather | solution.py:1277
  592.1 2.2 copy-done.1
  594.3 63.0 %shard_map.197 = f32[512,1024]{1,0:T(8,128)} custom-call(bf16[512,1024]{1,0:T(8,128)(2,1)S(1)} %convolution_convert_fusion.q_ref, bf16[4096,512]{1,0:T(8,128)(2,1)S(1)} %copy-done.1, bf16[4096,512]{1,0:T(8,128)(2,1)S(1)} %copy-done.1), custom_call_target="tpu_custom_call" | custom-call | flops 8999999488 | bytes 20000000 | tf_op jit(solution)/shard_map/pallas_call | solution.py:629
  657.3 0.0 copy-done.9
  657.3 1.3 copy.26
  (13 shorter events, 0.0 us)
Async XLA Ops:
  7.2 532.3 %copy-start = (bf16[4096,256]{1,0:T(8,128)(2,1)S(1)}, bf16[4096,256]{1,0:T(8,128)(2,1)}, u32[]{:S(2)}) copy-start(bf16[4096,256]{1,0:T(8,128)(2,1)} %param.37) | copy-start | bytes 6291460
  7.2 422.3 %all-gather.3.cloned.1.call-start = ((), (), s32[]{:S(2)}) async-start(), calls=%async_computation | async-start | bytes 18874368 | tf_op jit(solution)/shard_map/all_gather | solution.py:1249
  9.3 1.6 copy-start.2
  10.9 1.6 copy-start.3
  12.4 1.2 copy-start.4
  13.7 0.8 copy-start.5
  14.4 222.4 %copy-start.15 = (f32[32]{0:T(128)S(1)}, f32[32]{0:T(128)}, u32[]{:S(2)}) copy-start(f32[32]{0:T(128)} %param.31) | copy-start | bytes 388
  14.4 222.4 %copy-start.12 = (f32[32]{0:T(128)S(1)}, f32[32]{0:T(128)}, u32[]{:S(2)}) copy-start(f32[32]{0:T(128)} %param.30) | copy-start | bytes 388
  14.4 222.4 %copy-start.13 = (f32[32]{0:T(128)S(1)}, f32[32]{0:T(128)}, u32[]{:S(2)}) copy-start(f32[32]{0:T(128)} %param.29) | copy-start | bytes 388
  14.4 223.4 %copy-start.10 = (f32[4,256]{1,0:T(4,128)S(1)}, f32[4,256]{1,0:T(4,128)}, u32[]{:S(2)}) copy-start(f32[4,256]{1,0:T(4,128)} %param.28) | copy-start | bytes 12292
  14.4 223.4 %copy-start.11 = (f32[4,256]{1,0:T(4,128)S(1)}, f32[4,256]{1,0:T(4,128)}, u32[]{:S(2)}) copy-start(f32[4,256]{1,0:T(4,128)} %param.27) | copy-start | bytes 12292
  14.5 223.4 %copy-start.6 = (f32[2048]{0:T(1024)S(1)}, f32[2048]{0:T(1024)}, u32[]{:S(2)}) copy-start(f32[2048]{0:T(1024)} %param.32) | copy-start | bytes 24580
  234.1 2.6 copy-start.8
  236.7 355.4 %all-gather.5.cloned.1.call-start = ((), (), s32[]{:S(2)}) async-start(), calls=%async_computation.1 | async-start | bytes 4718592 | tf_op jit(solution)/shard_map/all_gather | solution.py:1277
  390.9 1.3 copy-start.7
  539.4 3.6 copy-start.14
  539.5 4.1 copy-start.16
  592.1 2.2 copy-start.1
  594.3 63.0 %copy-start.9 = (f32[512,1024]{1,0:T(8,128)S(1)}, f32[512,1024]{1,0:T(8,128)}, u32[]{:S(2)}) copy-start(f32[512,1024]{1,0:T(8,128)} %get-tuple-element.28) | copy-start | bytes 6291460
Sparse Core Ops, SparseCore 0:
  236.8 192.6 all-gather.2
  545.8 46.2 all-gather.4

commit v2 on v1

--- a/solution.py
+++ b/solution.py
@@ -650,6 +650,213 @@
     )(queries, pairs, pairs)
 
 
+def line_attention_kernel(
+    n,
+    nt_ref,
+    wq_ref,
+    wk_ref,
+    wv_ref,
+    o_ref,
+    keys,
+    values,
+    queries,
+    peak,
+    total,
+    acc,
+    send_sem,
+    recv_sem,
+):
+    me = lax.axis_index("seq")
+    chips = n // 2
+    z, c = me // 2, lax.rem(me, 2)
+    partner = 2 * z + 1 - c
+    rows = nt_ref.shape[0]
+    kv_heads = wk_ref.shape[1] // HD
+    per_kv = wq_ref.shape[1] // HD // kv_heads
+    factor = HD ** (-0.5) * math.log2(math.e)
+
+    barrier = pltpu.get_barrier_semaphore()
+    signal_seq(barrier, partner)
+    has_up, has_down = z + 1 <= chips - 1, z >= 1
+
+    @pl.when(has_up)
+    def _():
+        signal_seq(barrier, me + 2)
+
+    @pl.when(has_down)
+    def _():
+        signal_seq(barrier, me - 2)
+
+    inner_chip = jnp.logical_and(has_up, has_down)
+
+    @pl.when(inner_chip)
+    def _():
+        pl.semaphore_wait(barrier, 3)
+
+    @pl.when(jnp.logical_not(inner_chip))
+    def _():
+        pl.semaphore_wait(barrier, 2)
+
+    stores = (keys, values)
+
+    def copies(slot, kind, d, target):
+        return [
+            pltpu.make_async_remote_copy(
+                src_ref=store.at[slot],
+                dst_ref=store.at[slot],
+                send_sem=send_sem.at[kind, d, which],
+                recv_sem=recv_sem.at[kind, d, which],
+                device_id={"seq": target},
+                device_id_type=pl.DeviceIdType.MESH,
+            )
+            for which, store in enumerate(stores)
+        ]
+
+    def send(slot, kind, d, target):
+        for copy in copies(slot, kind, d, target):
+            copy.start()
+
+    def sent(slot, kind, d, target):
+        for copy in copies(slot, kind, d, target):
+            copy.wait_send()
+
+    def arrived(slot, kind, d):
+        for which, store in enumerate(stores):
+            place = store.at[slot]
+            pltpu.make_async_copy(place, place, recv_sem.at[kind, d, which]).wait()
+
+    keys[me] = jnp.dot(nt_ref[...], wk_ref[...], preferred_element_type=F32).astype(BF16)
+    values[me] = jnp.transpose(
+        jnp.dot(nt_ref[...], wv_ref[...], preferred_element_type=F32)
+    ).astype(BF16)
+
+    @pl.when(has_up)
+    def _():
+        send(me, 0, 1, me + 2)
+
+    @pl.when(c == 0)
+    def _():
+        send(me, 1, 0, partner)
+
+    tile = min(256, wq_ref.shape[1])
+    for at in range(0, wq_ref.shape[1], tile):
+        queries[:, at : at + tile] = jnp.dot(
+            nt_ref[...], wq_ref[:, at : at + tile], preferred_element_type=F32
+        ).astype(BF16)
+
+    def visit(block, first):
+        def group(g, carry_none):
+            lanes = pl.ds(pl.multiple_of(g * HD, HD), HD)
+            key = keys[block, :, lanes]
+            value = values[block, lanes, :]
+            for j in range(per_kv):
+                h = g * per_kv + j
+                query = queries[:, pl.ds(pl.multiple_of(h * HD, HD), HD)]
+                scores = lax.dot_general(
+                    key, query, (((1,), (1,)), ((), ())), preferred_element_type=F32
+                )
+                if first:
+                    row_id = lax.broadcasted_iota(jnp.int32, (rows, rows), 0)
+                    col_id = lax.broadcasted_iota(jnp.int32, (rows, rows), 1)
+                    scores = jnp.where(row_id <= col_id, scores, -1e30)
+                top = jnp.max(scores, axis=0, keepdims=True)
+                if not first:
+                    before = peak[h]
+                    top = jnp.maximum(before, top)
+                weights = jnp.exp2((scores - top) * factor)
+                added = jnp.sum(weights, axis=0, keepdims=True)
+                product = jnp.dot(value, weights.astype(BF16), preferred_element_type=F32)
+                if first:
+                    total[h] = added
+                    acc[h] = product
+                else:
+                    shrink = jnp.exp2((before - top) * factor)
+                    total[h] = total[h] * shrink + added
+                    acc[h] = acc[h] * shrink + product
+                peak[h] = top
+            return carry_none
+
+        lax.fori_loop(0, kv_heads, group, 0)
+
+    visit(me, True)
+
+    def earlier(t, carry_none):
+        d = (t + 1) // 2
+        mine = me - 2 * d
+        theirs = partner - 2 * d
+
+        @pl.when(lax.rem(t, 2) == 1)
+        def _():
+            arrived(mine, 0, d)
+
+            @pl.when(has_up)
+            def _():
+                send(mine, 0, d + 1, me + 2)
+
+            send(mine, 1, d, partner)
+
+        @pl.when(lax.rem(t, 2) == 0)
+        def _():
+            arrived(theirs, 1, d)
+
+        visit(partner - 2 * d + lax.rem(t, 2) * (me - partner), False)
+        return carry_none
+
+    lax.fori_loop(1 - c, 2 * z + 1, earlier, 0)
+
+    for h in range(kv_heads * per_kv):
+        o_ref[:, h * HD : (h + 1) * HD] = jnp.transpose(acc[h] / total[h])
+
+    @pl.when(has_up)
+    def _():
+        sent(me, 0, 1, me + 2)
+
+    @pl.when(c == 0)
+    def _():
+        sent(me, 1, 0, partner)
+
+    def flush(d, carry_none):
+        @pl.when(has_up)
+        def _():
+            sent(me - 2 * d, 0, d + 1, me + 2)
+
+        sent(me - 2 * d, 1, d, partner)
+        return carry_none
+
+    lax.fori_loop(1, z + 1, flush, 0)
+
+
+def line_attention(normed_two, w_q, w_k, w_v):
+    n = lax.axis_size("seq")
+    rows = normed_two.shape[0]
+    heads = w_q.shape[1] // HD
+    wide = w_k.shape[1]
+    chips = n // 2
+    vmem = pl.BlockSpec(memory_space=pltpu.VMEM)
+    return pl.pallas_call(
+        functools.partial(line_attention_kernel, n),
+        out_shape=jax.ShapeDtypeStruct((rows, w_q.shape[1]), F32),
+        in_specs=[vmem] * 4,
+        out_specs=vmem,
+        scratch_shapes=[
+            pltpu.VMEM((n, rows, wide), BF16),
+            pltpu.VMEM((n, wide, rows), BF16),
+            pltpu.VMEM((rows, w_q.shape[1]), BF16),
+            pltpu.VMEM((heads, 1, rows), F32),
+            pltpu.VMEM((heads, 1, rows), F32),
+            pltpu.VMEM((heads, HD, rows), F32),
+            pltpu.SemaphoreType.DMA((2, chips, 2)),
+            pltpu.SemaphoreType.DMA((2, chips, 2)),
+        ],
+        compiler_params=pltpu.CompilerParams(
+            collective_id=5, has_side_effects=True, vmem_limit_bytes=56 * 1024 * 1024
+        ),
+        cost_estimate=pl.CostEstimate(
+            flops=18_000_000_000, bytes_accessed=30_000_000, transcendentals=17_000_000
+        ),
+    )(normed_two, w_q, w_k, w_v)
+
+
 def pad_lanes(values):
     return jnp.pad(values, ((0, 0), (0, LANES - values.shape[1])))
 
@@ -755,12 +962,15 @@
             )
         send(cond, lambda: (wdt_ref, dt_ref.at[:, here]), ("dt", way, d, same), seq=target)
 
-    def weights_at(d):
-        for way in (1, -1):
-            chip = z + way * d
-            cond = chip <= chips - 1 if way == 1 else chip >= 0
-            for same in (True, False):
-                send_weights(way, d, same, cond, chip)
+    def weights_at(t):
+        for d in range(1, chips - (t if t > 1 else 0)):
+            for way in (1, -1):
+                chip = z + way * d
+                behind = z if way == 1 else chips - 1 - z
+                now = behind <= 1 if t == 1 else behind == t
+                cond = both(now, chip <= chips - 1 if way == 1 else chip >= 0)
+                for same in (True, False):
+                    send_weights(way, d, same, cond, chip)
 
     send_weights(0, 0, False, True, z)
     here = pl.ds(pl.multiple_of(me * depth, depth), depth)
@@ -875,8 +1085,8 @@
     for t in range(chips + 2):
         if t <= last:
             step(stage_a, t)
-            if last - t >= 1:
-                weights_at(last - t)
+            if 1 <= t < last:
+                weights_at(t)
         if 0 <= t - 1 <= last:
             step(stage_b, t - 1)
         if 0 <= t - 2 <= last:
@@ -941,7 +1151,7 @@
             pltpu.VMEM((rows, LANES), F32),
             pltpu.VMEM((4, 8, rows), F32),
             pltpu.SemaphoreType.DMA((5,)),
-            pltpu.SemaphoreType.DMA((45 * n // 2,)),
+            pltpu.SemaphoreType.DMA((50 * n // 2,)),
             pltpu.SemaphoreType.DMA((30 * n // 2,)),
         ],
         compiler_params=pltpu.CompilerParams(
@@ -964,7 +1174,10 @@
     rate_ref,
     skip_ref,
     gain_ref,
+    wout_ref,
     y_ref,
+    rows_ref,
+    held_ref,
     blocks,
     wdt_own,
     window,
@@ -973,12 +1186,28 @@
     conv,
     state,
     out,
-    landed,
+    normed,
+    power,
     load_sem,
-    send_sem,
-    recv_sem,
+    local_sem,
+    power_send,
+    power_recv,
+    plane_send,
+    plane_recv,
+    wout_send,
+    wout_recv,
 ):
     me = lax.axis_index("seq")
+    member = lax.axis_index("mp")
+    m = lax.axis_size("mp")
+    chips = n // 2
+    z, c = me // 2, lax.rem(me, 2)
+    partner = 2 * z + 1 - c
+    per = n // groups
+    base = me // per * per
+    place = member * 2 + c
+    quarter = 2 * gate.shape[1]
+    strip = wout_ref.shape[1]
     rows = blocks.shape[1]
     inner = gate.shape[1]
     width = inner + 2 * N
@@ -988,7 +1217,63 @@
     barrier = pltpu.get_barrier_semaphore()
     for d in range(1, n):
         signal_seq(barrier, lax.rem(me + d, n))
-    pl.semaphore_wait(barrier, n - 1)
+    for d in range(1, m):
+        for core in range(2):
+            pl.semaphore_signal(
+                barrier,
+                inc=1,
+                device_id={"mp": lax.rem(member + d, m), "seq": 2 * z + core},
+                device_id_type=pl.DeviceIdType.MESH,
+            )
+    pl.semaphore_wait(barrier, n - 1 + 2 * (m - 1))
+
+    def remote(source, target_ref, sends, recvs, **target):
+        return pltpu.make_async_remote_copy(
+            src_ref=source,
+            dst_ref=target_ref,
+            send_sem=sends,
+            recv_sem=recvs,
+            device_id=target,
+            device_id_type=pl.DeviceIdType.MESH,
+        )
+
+    def landed(target_ref, recvs):
+        pltpu.make_async_copy(target_ref, target_ref, recvs).wait()
+
+    def own_rows(chip):
+        return wout_ref.at[pl.ds(pl.multiple_of(chip * quarter, quarter), quarter), :]
+
+    def first_leg(d):
+        chip = lax.rem(z + d, chips)
+        return remote(
+            own_rows(chip), held_ref.at[z], wout_send.at[0, d], wout_recv.at[0, d], seq=2 * chip + c
+        )
+
+    def second_place(of):
+        return rows_ref.at[
+            pl.ds(pl.multiple_of(of * quarter, quarter), quarter),
+            pl.ds(pl.multiple_of(c * strip, strip), strip),
+        ]
+
+    def second_leg(d):
+        q = lax.rem(member + d, m)
+        return remote(
+            held_ref.at[q], second_place(member), wout_send.at[1, d], wout_recv.at[1, d], mp=q
+        )
+
+    def third_leg(d):
+        of = second_place(lax.rem(member + d, m))
+        return remote(of, of, wout_send.at[2, d], wout_recv.at[2, d], seq=partner)
+
+    def keep_held():
+        return pltpu.make_async_copy(own_rows(z), held_ref.at[z], local_sem.at[0])
+
+    def keep_rows():
+        return pltpu.make_async_copy(held_ref.at[member], second_place(member), local_sem.at[1])
+
+    for d in range(1, chips):
+        first_leg(d).start()
+    keep_held().start()
 
     def load(i, slot):
         return pltpu.make_async_copy(
@@ -1018,15 +1303,58 @@
     low_lanes = col_id < P_SIZE
     tri = jnp.where(causal, 1.0, 0.0).astype(F32)
 
-    def hand_over(i):
-        return pltpu.make_async_remote_copy(
-            src_ref=out.at[i],
-            dst_ref=landed.at[me],
-            send_sem=send_sem.at[i],
-            recv_sem=recv_sem.at[me],
-            device_id={"seq": i},
-            device_id_type=pl.DeviceIdType.MESH,
-        )
+    def tell(i, k):
+        target = base + lax.rem(me - base + k, per)
+        return remote(
+            power.at[i, 0], power.at[i, k], power_send.at[i, k], power_recv.at[i, k], seq=target
+        )
+
+    def spot(i, at):
+        return y_ref.at[i // 2, :, pl.ds(pl.multiple_of(at * inner, inner), inner)]
+
+    def to_plane(i, d):
+        return remote(
+            normed.at[i],
+            spot(i, place),
+            plane_send.at[i, d],
+            plane_recv.at[i // 2, place],
+            mp=lax.rem(member + d, m),
+            seq=2 * z + lax.rem(i, 2),
+        )
+
+    def to_partner(i):
+        return remote(
+            normed.at[i],
+            spot(i, place),
+            plane_send.at[i, 0],
+            plane_recv.at[i // 2, place],
+            seq=partner,
+        )
+
+    def to_self(i):
+        return pltpu.make_async_copy(normed.at[i], spot(i, place), plane_send.at[i, 0])
+
+    def finish(i):
+        for k in range(1, per):
+            landed(power.at[i, k], power_recv.at[i, k])
+        sums = power[i, 0]
+        for k in range(1, per):
+            sums = sums + power[i, k]
+        column = jnp.transpose(jnp.broadcast_to(sums[0:1, :], (LANES, rows)))
+        for sub in range(rows // QB):
+            here = slice(sub * QB, (sub + 1) * QB)
+            scale = lax.rsqrt(column[here, 0:1] / (per * inner) + 1e-05)
+            normed[i, here, :] = (out[i, here, :].astype(F32) * scale * gain_ref[...]).astype(BF16)
+        for d in range(1, m):
+            to_plane(i, d).start()
+
+        @pl.when(lax.rem(i, 2) == c)
+        def _():
+            to_self(i).start()
+
+        @pl.when(lax.rem(i, 2) != c)
+        def _():
+            to_partner(i).start()
 
     def block(i, carry_none):
         slot = lax.rem(i, 2)
@@ -1047,6 +1375,11 @@
         raws[...] = lax.dot_general(
             source[...], wdt_own[...], (((1,), (1,)), ((), ())), preferred_element_type=F32
         )
+
+        @pl.when(i > 0)
+        def _():
+            finish(i - 1)
+
         for sub in range(rows // QB):
             at = sub * QB
             here = slice(at, at + QB)
@@ -1079,6 +1412,7 @@
             affinity = lax.dot_general(c, b, (((1,), (1,)), ((), ())), preferred_element_type=F32)
             affinity = jnp.where(causal, affinity, 0.0)
             full = carried + skip_ref[...] * x
+            squares = None
             for pair in range(inner // LANES):
                 lanes = slice(pair * LANES, (pair + 1) * LANES)
                 outs = []
@@ -1090,67 +1424,95 @@
                         jnp.dot(mixing, scaled_low[:, lanes], preferred_element_type=F32)
                     )
                 inside = jnp.where(low_lanes, outs[0], outs[1])
-                out[i, here, lanes] = (
-                    (full[:, lanes] + inside) * silu(gate[here, lanes])
-                ).astype(BF16)
+                gated = (full[:, lanes] + inside) * silu(gate[here, lanes])
+                out[i, here, lanes] = gated.astype(BF16)
+                squares = gated * gated if squares is None else squares + gated * gated
+            totals = jnp.broadcast_to(jnp.sum(squares, axis=-1, keepdims=True), (QB, LANES))
+            power[i, 0, :, here] = jnp.transpose(totals)[0:8, :]
         window[0:8, :] = window[rows : rows + 8, :]
 
-        @pl.when(i != me)
+        for k in range(1, per):
+            tell(i, k).start()
+
+        @pl.when(i == n // 2)
         def _():
-            hand_over(i).start()
+            keep_held().wait()
+            for d in range(1, chips):
+                landed(held_ref.at[lax.rem(z + d, chips)], wout_recv.at[0, chips - d])
+            keep_rows().start()
+            for d in range(1, m):
+                second_leg(d).start()
+
+        @pl.when(i == n - 2)
+        def _():
+            keep_rows().wait()
+            third_leg(0).start()
+            for d in range(1, m):
+                landed(second_place(lax.rem(member + d, m)), wout_recv.at[1, m - d])
+                third_leg(d).start()
 
         return carry_none
 
     lax.fori_loop(0, n, block, 0)
-
-    for s in range(n):
-
-        @pl.when(s != me)
+    finish(n - 1)
+    for d in range(m):
+        strips = pl.ds(pl.multiple_of((1 - c) * strip, strip), strip)
+        of = lax.rem(member + d, m)
+        landed(
+            rows_ref.at[pl.ds(pl.multiple_of(of * quarter, quarter), quarter), strips],
+            wout_recv.at[2, d],
+        )
+    for j in range(chips):
+        for at in range(2 * m):
+
+            @pl.when(at != place)
+            def _():
+                landed(y_ref.at[j, :, at * inner : (at + 1) * inner], plane_recv.at[j, at])
+
+    def flush(i, carry_none):
+        for k in range(1, per):
+            tell(i, k).wait_send()
+        for d in range(1, m):
+            to_plane(i, d).wait_send()
+
+        @pl.when(lax.rem(i, 2) == c)
         def _():
-            pltpu.make_async_copy(landed.at[s], landed.at[s], recv_sem.at[s]).wait()
-
-        @pl.when(s == me)
+            to_self(i).wait()
+
+        @pl.when(lax.rem(i, 2) != c)
         def _():
-            landed[s] = out[s]
-
-    per = n // groups
-    for g in range(groups):
-        members = range(g * per, (g + 1) * per)
-
-        def finish(i, carry_none):
-            at = pl.ds(pl.multiple_of(i * QB, QB), QB)
-            power = None
-            for s in members:
-                v = landed[s, at, :].astype(F32)
-                part = jnp.sum(v * v, axis=-1, keepdims=True)
-                power = part if power is None else power + part
-            scale = lax.rsqrt(power / (per * inner) + 1e-05)
-            for s in members:
-                lanes = slice(s * inner, (s + 1) * inner)
-                v = landed[s, at, :].astype(F32)
-                y_ref[at, lanes] = (v * scale * gain_ref[:, lanes]).astype(BF16)
-            return carry_none
-
-        lax.fori_loop(0, rows // QB, finish, 0)
-    for s in range(n):
-
-        @pl.when(s != me)
-        def _():
-            hand_over(s).wait_send()
-
-
-def mix_heads(hidden, weights, w_dt, taps, bias, rate, skip, gain, groups):
-    n = lax.axis_size("seq")
+            to_partner(i).wait_send()
+
+        return carry_none
+
+    lax.fori_loop(0, n, flush, 0)
+    for d in range(1, chips):
+        first_leg(d).wait_send()
+    for d in range(1, m):
+        second_leg(d).wait_send()
+    for d in range(m):
+        third_leg(d).wait_send()
+
+
+def mix_heads(hidden, w_out, weights, w_dt, taps, bias, rate, skip, gain, groups):
+    n, m = lax.axis_size("seq"), lax.axis_size("mp")
     rows = hidden.shape[0] // n
     features = hidden.shape[1]
     inner = skip.shape[1]
     width = inner + 2 * N
+    quarter, strip = 2 * inner, w_out.shape[1]
+    per = n // groups
     vmem = pl.BlockSpec(memory_space=pltpu.VMEM)
+    anywhere = pl.BlockSpec(memory_space=pl.ANY)
     return pl.pallas_call(
         functools.partial(heads_kernel, n, groups),
-        out_shape=jax.ShapeDtypeStruct((rows, n * inner), BF16),
-        in_specs=[pl.BlockSpec(memory_space=pl.ANY)] + [vmem] * 7,
-        out_specs=vmem,
+        out_shape=(
+            jax.ShapeDtypeStruct((n // 2, rows, 2 * m * inner), BF16),
+            jax.ShapeDtypeStruct((m * quarter, 2 * strip), BF16),
+            jax.ShapeDtypeStruct((n // 2, quarter, strip), BF16),
+        ),
+        in_specs=[anywhere] + [vmem] * 7 + [anywhere],
+        out_specs=(anywhere,) * 3,
         scratch_shapes=[
             pltpu.VMEM((2, rows, features), BF16),
             pltpu.VMEM((LANES, features), BF16),
@@ -1161,9 +1523,15 @@
             pltpu.VMEM((N, inner), F32),
             pltpu.VMEM((n, rows, inner), BF16),
             pltpu.VMEM((n, rows, inner), BF16),
+            pltpu.VMEM((n, per, 8, rows), F32),
             pltpu.SemaphoreType.DMA((2,)),
-            pltpu.SemaphoreType.DMA((n,)),
-            pltpu.SemaphoreType.DMA((n,)),
+            pltpu.SemaphoreType.DMA((2,)),
+            pltpu.SemaphoreType.DMA((n, per)),
+            pltpu.SemaphoreType.DMA((n, per)),
+            pltpu.SemaphoreType.DMA((n, m)),
+            pltpu.SemaphoreType.DMA((n // 2, 2 * m)),
+            pltpu.SemaphoreType.DMA((3, m)),
+            pltpu.SemaphoreType.DMA((3, m)),
         ],
         compiler_params=pltpu.CompilerParams(
             collective_id=4, has_side_effects=True, vmem_limit_bytes=48 * 1024 * 1024
@@ -1171,7 +1539,212 @@
         cost_estimate=pl.CostEstimate(
             flops=40_000_000_000, bytes_accessed=50_000_000, transcendentals=8_000_000
         ),
-    )(hidden, weights, w_dt, taps, bias, rate, skip, gain)
+    )(hidden, weights, w_dt, taps, bias, rate, skip, gain, w_out)
+
+
+def combine_kernel(
+    n,
+    y_ref,
+    w_ref,
+    hidden_ref,
+    gain_ref,
+    mixed_ref,
+    normed_ref,
+    part,
+    outgoing,
+    incoming,
+    low,
+    send_sem,
+    recv_sem,
+    own_sem,
+    mp_send,
+    mp_recv,
+):
+    me = lax.axis_index("seq")
+    member = lax.axis_index("mp")
+    chips = n // 2
+    z = me // 2
+    across = member + 1 - 2 * lax.rem(member, 2)
+    along = lax.rem(member + 2, 4)
+    far = 3 - member
+    rows, wide = hidden_ref.shape
+    tile = part.shape[1]
+    tiles = wide // tile
+    has_up, has_down = z + 1 <= chips - 1, z >= 1
+
+    barrier = pltpu.get_barrier_semaphore()
+    signal_mp(barrier, across)
+    signal_mp(barrier, along)
+
+    @pl.when(has_up)
+    def _():
+        signal_seq(barrier, me + 2)
+
+    @pl.when(has_down)
+    def _():
+        signal_seq(barrier, me - 2)
+
+    ends = jnp.logical_and(has_up, has_down)
+
+    @pl.when(ends)
+    def _():
+        pl.semaphore_wait(barrier, 4)
+
+    @pl.when(jnp.logical_not(ends))
+    def _():
+        pl.semaphore_wait(barrier, 3)
+
+    def hand_on(j, t, way):
+        here = slice(t * tile, (t + 1) * tile)
+        return pltpu.make_async_remote_copy(
+            src_ref=outgoing.at[j, :, here],
+            dst_ref=incoming.at[way, j, :, here],
+            send_sem=send_sem.at[j, t],
+            recv_sem=recv_sem.at[way, j, t],
+            device_id={"seq": me + 2 if way == 0 else me - 2},
+            device_id_type=pl.DeviceIdType.MESH,
+        )
+
+    def take(j, t, way):
+        here = slice(t * tile, (t + 1) * tile)
+        where = incoming.at[way, j, :, here]
+        pltpu.make_async_copy(where, where, recv_sem.at[way, j, t]).wait()
+        return incoming[way, j, :, here].astype(F32)
+
+    order = []
+    for k in range((chips + 1) // 2):
+        order += [chips - 1 - k] + ([k] if k != chips - 1 - k else [])
+    for j in order:
+        for t in range(tiles):
+            here = slice(t * tile, (t + 1) * tile)
+
+            @pl.when(z != j)
+            def _():
+                part[...] = jnp.dot(y_ref[j], w_ref[:, here], preferred_element_type=F32)
+
+            @pl.when(jnp.logical_and(z < j, z >= 1))
+            def _():
+                part[...] += take(j, t, 0)
+
+            @pl.when(jnp.logical_and(z > j, z <= chips - 2))
+            def _():
+                part[...] += take(j, t, 1)
+
+            @pl.when(z != j)
+            def _():
+                outgoing[j, :, here] = part[...].astype(BF16)
+
+            @pl.when(z < j)
+            def _():
+                hand_on(j, t, 0).start()
+
+            @pl.when(z > j)
+            def _():
+                hand_on(j, t, 1).start()
+
+    for t in range(tiles):
+        here = slice(t * tile, (t + 1) * tile)
+        mixed_ref[:, here] = hidden_ref[:, here].astype(F32) + jnp.dot(
+            y_ref[z], w_ref[:, here], preferred_element_type=F32
+        )
+    for t in range(tiles):
+        here = slice(t * tile, (t + 1) * tile)
+
+        @pl.when(has_down)
+        def _():
+            mixed_ref[:, here] += take(z, t, 0)
+
+        @pl.when(has_up)
+        def _():
+            mixed_ref[:, here] += take(z, t, 1)
+
+        low[:, here] = mixed_ref[:, here].astype(BF16)
+
+    def feature(owner, half=None):
+        at = pl.ds(pl.multiple_of(owner * wide, wide), wide)
+        if half is None:
+            return normed_ref.at[:, at]
+        return normed_ref.at[half * (rows // 2) : (half + 1) * (rows // 2), at]
+
+    def share(index, source, place, target):
+        return pltpu.make_async_remote_copy(
+            src_ref=source,
+            dst_ref=place,
+            send_sem=mp_send.at[index],
+            recv_sem=mp_recv.at[index],
+            device_id={"mp": target},
+            device_id_type=pl.DeviceIdType.MESH,
+        )
+
+    def arrived(index, place):
+        pltpu.make_async_copy(place, place, mp_recv.at[index]).wait()
+
+    shared = [
+        share(0, low, feature(member), across),
+        share(1, low, feature(member), along),
+        share(2, feature(across, 0), feature(across, 0), along),
+        share(3, feature(along, 1), feature(along, 1), across),
+    ]
+    shared[0].start()
+    shared[1].start()
+    own_copy = pltpu.make_async_copy(low, feature(member), own_sem)
+    own_copy.start()
+    arrived(0, feature(across))
+    shared[2].start()
+    arrived(1, feature(along))
+    shared[3].start()
+    arrived(2, feature(far, 0))
+    arrived(3, feature(far, 1))
+    own_copy.wait()
+    for copy in shared:
+        copy.wait_send()
+    norm_rows(normed_ref, gain_ref, normed_ref)
+    for j in range(chips):
+        for t in range(tiles):
+
+            @pl.when(z < j)
+            def _():
+                hand_on(j, t, 0).wait_send()
+
+            @pl.when(z > j)
+            def _():
+                hand_on(j, t, 1).wait_send()
+
+
+def combine(y, weights, hidden, gain):
+    n = lax.axis_size("seq")
+    rows, wide = hidden.shape
+    chips = n // 2
+    tile = min(256, wide)
+    vmem = pl.BlockSpec(memory_space=pltpu.VMEM)
+    return pl.pallas_call(
+        functools.partial(combine_kernel, n),
+        out_shape=(
+            jax.ShapeDtypeStruct((rows, wide), F32),
+            jax.ShapeDtypeStruct((rows, 4 * wide), BF16),
+        ),
+        in_specs=[vmem] * 4,
+        out_specs=(vmem, vmem),
+        scratch_shapes=[
+            pltpu.VMEM((rows, tile), F32),
+            pltpu.VMEM((chips, rows, wide), BF16),
+            pltpu.VMEM((2, chips, rows, wide), BF16),
+            pltpu.VMEM((rows, wide), BF16),
+            pltpu.SemaphoreType.DMA((chips, wide // tile)),
+            pltpu.SemaphoreType.DMA((2, chips, wide // tile)),
+            pltpu.SemaphoreType.DMA,
+            pltpu.SemaphoreType.DMA((4,)),
+            pltpu.SemaphoreType.DMA((4,)),
+        ],
+        compiler_params=pltpu.CompilerParams(
+            collective_id=6, has_side_effects=True, vmem_limit_bytes=56 * 1024 * 1024
+        ),
+        cost_estimate=pl.CostEstimate(
+            flops=2 * chips * rows * y.shape[2] * wide,
+            bytes_accessed=60_000_000,
+            transcendentals=0,
+        ),
+    )(y, weights, hidden, gain)
 
 
 def own_slice(values, index, size):
@@ -1207,7 +1780,7 @@
         bias=pad_lanes(own_slice(dt_bias[None, :], me, heads)),
         rate=pad_lanes(own_slice(a_rate[None, :], me, heads)),
         skip=jnp.repeat(own_slice(skip_gain[None, :], me, heads), P_SIZE, axis=1),
-        gain=group_gain[None, :],
+        gain=own_slice(group_gain[None, :], me, inner),
         groups=groups,
     )
 
@@ -1216,7 +1789,7 @@
     n, m = lax.axis_size("seq"), lax.axis_size("mp")
     groups = conv_b.shape[1] // N
     whole = conv_x.shape[1] % (n * LANES) == 0 and n % groups == 0
-    return m == 4 and n % 2 == 0 and n >= 4 and whole
+    return m == 4 and n == 2 * m and whole
 
 
 def on_device(
@@ -1245,9 +1818,8 @@
             hidden_in, norm_gain, w_z, w_x, w_b, w_c, w_dt, conv_x, conv_b, conv_c, dt_bias,
             a_rate, skip_gain, group_gain,
         )
-        hidden, w_out = lax.optimization_barrier((hidden, w_out))
-        out_columns = lax.all_gather(w_out, "seq", axis=1, tiled=True)
-        y_normed = mix(hidden)
+        y_normed, out_rows, _ = mix(hidden, w_out)
+        mixed, normed_two = combine(y_normed, out_rows, hidden_in, attn_gain[None, :])
     else:
         proj = gather_dot(
             hidden_in,
@@ -1271,14 +1843,20 @@
             heads,
             groups,
         )
-    mixed, normed_two = output_stage(y_normed, out_columns, hidden_in, attn_gain[None, :])
-    own_keys = jnp.dot(normed_two, w_k, preferred_element_type=F32).astype(BF16)
-    own_values = jnp.dot(normed_two, w_v, preferred_element_type=F32).astype(BF16)
-    pairs = lax.all_gather(
-        jnp.concatenate([own_keys, own_values], axis=1), "seq", axis=0, tiled=True
-    )
-    queries = jnp.dot(normed_two, w_q, preferred_element_type=F32).astype(BF16)
-    context = attention(queries, pairs, own_keys.shape[1] // HD)
+        mixed, normed_two = output_stage(
+            y_normed, out_columns, hidden_in, attn_gain[None, :]
+        )
+    n = lax.axis_size("seq")
+    if n % 2 == 0 and n >= 4 and WINDOW >= n * hidden_in.shape[0]:
+        context = line_attention(normed_two, w_q, w_k, w_v)
+    else:
+        own_keys = jnp.dot(normed_two, w_k, preferred_element_type=F32).astype(BF16)
+        own_values = jnp.dot(normed_two, w_v, preferred_element_type=F32).astype(BF16)
+        pairs = lax.all_gather(
+            jnp.concatenate([own_keys, own_values], axis=1), "seq", axis=0, tiled=True
+        )
+        queries = jnp.dot(normed_two, w_q, preferred_element_type=F32).astype(BF16)
+        context = attention(queries, pairs, own_keys.shape[1] // HD)
     return (mixed, context)
 
 

time: 666 us -> 536 us (0.80)
  waiting for transfers between devices: 74.6 us -> 0 us
  Pallas kernels: 546 us -> 520 us
  matrix products: 14 us -> 0 us
  between operations: 14.2 us -> 0.8 us
    all_gather x2 -> x0, waiting for transfers between devices: 74.6 us -> none  [the longest x1 37.3 us: on_device(): lax.all_gather(jnp.concatenate([own_keys, own_values], axis=1), 'seq', ax...]
    pallas_call x1, Pallas kernels: 220 us -> 177 us  [spread(): pl.pallas_call(functools.partial(spread_kernel, n, groups), out_shape=(ja...]
    pallas_call x3, Pallas kernels: 326 us -> 343 us  [the longest x1 156 us: mix_heads(): pl.pallas_call(functools.partial(heads_kernel, n, groups), out_shape=(jax...]
    dot_general x3 -> x0, matrix products: 14 us -> none  [the longest x1 9.15 us: on_device(): queries = jnp.dot(normed_two, w_q, preferred_element_type=F32).astype(BF16)]
  transfers between devices with their start and end apart: 2 -> 0, of which waited for: 2 -> 0; matrix products, arithmetic and copies ran while one was open for 2% -> 0% of each run, Pallas kernels for 23% -> 0%
where the time goes in v2:
time: 536 us; the launch traced here: 535 us
  Pallas kernels  520 us (97%)
  local copies, waits for them, and re-layouts  14.3 us (3%)
    pallas_call x1, Pallas kernels, spread(): pl.pallas_call(functools.partial(spread_kernel, n, groups), out_shape=(ja...  177 us
    pallas_call x1, Pallas kernels, mix_heads(): pl.pallas_call(functools.partial(heads_kernel, n, groups), out_shape=(jax...  156 us
    pallas_call x1, Pallas kernels, line_attention(): pl.pallas_call(functools.partial(line_attention_kernel, n), out_shape=jax...  100 us
    pallas_call x1, Pallas kernels, combine(): pl.pallas_call(functools.partial(combine_kernel, n), out_shape=(jax.Shape...  86.1 us

profile of v2, /device:TPU:25, one launch (start us, length us, event | category | flops | bytes accessed | tf_op | source)
XLA Modules:
  0.0 534.7 jit_solution(6393277837053048672)
XLA Ops:
  0.6 0.0 copy-start
  0.6 0.0 copy-start.6
  0.7 0.0 copy-start.2
  0.7 0.9 dynamic-slice.18
  1.6 0.7 dynamic-slice_bitcast_fusion
  2.3 0.8 dynamic-slice.19
  3.1 0.1 broadcast_in_dim.6
  3.2 0.1 broadcast_in_dim.14.skip_ref
  3.3 0.0 copy-done
  3.3 0.7 dynamic-slice.15
  3.9 0.7 constant_dynamic-slice_fusion
  4.7 1.1 fusion
  5.8 0.1 pad_maximum_fusion.wbc_ref
  5.8 0.0 copy-done.6
  5.9 0.0 copy-done.2
  5.9 0.0 copy-start.3
  5.9 1.6 copy-done.3
  7.5 0.0 copy-start.5
  7.5 1.2 copy-done.5
  8.7 0.0 copy-start.4
  8.7 176.7 %shard_map.194 = (bf16[4096,4096]{1,0:T(8,128)(2,1)}, bf16[4096,768]{1,0:T(8,128)(2,1)S(1)}, bf16[32,4096]{1,0:T(8,128)(2,1)S(1)}) custom-call(bf16[512,1024]{1,0:T(8,128)(2,1)S(1)} %copy-done.5, f32[1,1024]{1,0:T(1,128)S(1)} %bitcast.8, bf16[512,2048]{1,0:T(8,128)(2,1)S(1)} %copy-done.2, bf16[512,2048]{1,0:T(8,128)(2,1)S(1)} %copy-done.3, ...), custom_call_target="tpu_custom_call" | custom-call | flops 20000000000 | bytes 100000000 | tf_op jit(solution)/shard_map/pallas_call | solution.py:1140
  185.4 0.0 copy-start.7
  185.4 2.7 copy-done.7
  188.1 0.0 copy-done.4
  188.1 156.4 %shard_map.195 = (bf16[4,512,2048]{2,1,0:T(8,128)(2,1)}, bf16[2048,1024]{1,0:T(8,128)(2,1)}, bf16[4,512,512]{2,1,0:T(8,128)(2,1)}) custom-call(bf16[4096,4096]{1,0:T(8,128)(2,1)} %get-tuple-element.9.hidden_ref, bf16[4096,768]{1,0:T(8,128)(2,1)} %copy-done.7, bf16[32,4096]{1,0:T(8,128)(2,1)S(1)} %get-tuple-element.11.wdt_ref, ...), custom_call_target="tpu_custom_call" | custom-call | flops 40000000000 | bytes 50000000 | tf_op jit(solution)/shard_map/pallas_call | solution.py:1507
  344.5 86.1 %shard_map.196 = (f32[512,1024]{1,0:T(8,128)}, bf16[512,4096]{1,0:T(8,128)(2,1)}) custom-call(bf16[4,512,2048]{2,1,0:T(8,128)(2,1)} %get-tuple-element.12.y_ref, bf16[2048,1024]{1,0:T(8,128)(2,1)} %get-tuple-element.13.w_ref, bf16[512,1024]{1,0:T(8,128)(2,1)} %hidden_ref.3, f32[1,4096]{1,0:T(1,128)} %bitcast.11), custom_call_target="tpu_custom_call" | custom-call | flops 8589934592 | bytes 60000000 | tf_op jit(solution)/shard_map/pallas_call | solution.py:1720
  430.6 0.0 copy-start.8
  430.6 100.4 %shard_map.197 = f32[512,1024]{1,0:T(8,128)} custom-call(bf16[512,4096]{1,0:T(8,128)(2,1)} %get-tuple-element.15.nt_ref, bf16[4096,1024]{1,0:T(8,128)(2,1)} %wq_ref.1, bf16[4096,256]{1,0:T(8,128)(2,1)} %wk_ref.1, bf16[4096,256]{1,0:T(8,128)(2,1)} %wv_ref.1), custom_call_target="tpu_custom_call" | custom-call | flops 17999998976 | bytes 30000000 | tf_op jit(solution)/shard_map/pallas_call | solution.py:836
  531.0 0.0 copy-done.8
  531.0 0.0 copy-start.9
  531.0 0.0 copy-start.1
  531.0 1.3 copy.23
  532.4 1.0 copy-done.9
  533.4 1.3 copy.24
  534.7 0.0 copy-done.1
  (4 shorter events, 0.0 us)
Async XLA Ops:
  0.6 2.6 copy-start
  0.6 5.2 copy-start.6
  0.7 5.2 copy-start.2
  5.9 1.6 copy-start.3
  7.5 1.2 copy-start.5
  8.7 179.4 %copy-start.4 = (bf16[2048,512]{1,0:T(8,128)(2,1)S(1)}, bf16[2048,512]{1,0:T(8,128)(2,1)}, u32[]{:S(2)}) copy-start(bf16[2048,512]{1,0:T(8,128)(2,1)} %wout_ref.1) | copy-start | bytes 6291460
  185.4 2.7 copy-start.7
  430.6 100.4 %copy-start.8 = (f32[512,1024]{1,0:T(8,128)S(1)}, f32[512,1024]{1,0:T(8,128)}, u32[]{:S(2)}) copy-start(f32[512,1024]{1,0:T(8,128)} %get-tuple-element.28) | copy-start | bytes 6291460
  531.0 2.3 copy-start.9
  531.0 3.7 copy-start.1

commit v3 on v2

--- a/solution.py
+++ b/solution.py
@@ -1194,6 +1194,9 @@
     power_recv,
     plane_send,
     plane_recv,
+    relay_send,
+    first_send,
+    first_recv,
     wout_send,
     wout_recv,
 ):
@@ -1208,6 +1211,9 @@
     place = member * 2 + c
     quarter = 2 * gate.shape[1]
     strip = wout_ref.shape[1]
+    across = member + 1 - 2 * lax.rem(member, 2)
+    along = lax.rem(member + 2, 4)
+    far = 3 - member
     rows = blocks.shape[1]
     inner = gate.shape[1]
     width = inner + 2 * N
@@ -1243,10 +1249,17 @@
     def own_rows(chip):
         return wout_ref.at[pl.ds(pl.multiple_of(chip * quarter, quarter), quarter), :]
 
-    def first_leg(d):
+    parts = first_send.shape[0]
+    slim = quarter // parts
+
+    def first_leg(d, q):
         chip = lax.rem(z + d, chips)
         return remote(
-            own_rows(chip), held_ref.at[z], wout_send.at[0, d], wout_recv.at[0, d], seq=2 * chip + c
+            wout_ref.at[pl.ds(pl.multiple_of(chip * quarter + q * slim, slim), slim), :],
+            held_ref.at[z, pl.ds(pl.multiple_of(q * slim, slim), slim), :],
+            first_send.at[q, d],
+            first_recv.at[q, d],
+            seq=2 * chip + c,
         )
 
     def second_place(of):
@@ -1271,8 +1284,6 @@
     def keep_rows():
         return pltpu.make_async_copy(held_ref.at[member], second_place(member), local_sem.at[1])
 
-    for d in range(1, chips):
-        first_leg(d).start()
     keep_held().start()
 
     def load(i, slot):
@@ -1309,16 +1320,18 @@
             power.at[i, 0], power.at[i, k], power_send.at[i, k], power_recv.at[i, k], seq=target
         )
 
-    def spot(i, at):
-        return y_ref.at[i // 2, :, pl.ds(pl.multiple_of(at * inner, inner), inner)]
-
-    def to_plane(i, d):
+    def spot(i, at, half=None):
+        if half is None:
+            return y_ref.at[i // 2, at]
+        return y_ref.at[i // 2, at, half * (rows // 2) : (half + 1) * (rows // 2), :]
+
+    def to_plane(i, k):
         return remote(
             normed.at[i],
             spot(i, place),
-            plane_send.at[i, d],
-            plane_recv.at[i // 2, place],
-            mp=lax.rem(member + d, m),
+            plane_send.at[i, k + 1],
+            plane_recv.at[i // 2, place, 0],
+            mp=(across, along)[k],
             seq=2 * z + lax.rem(i, 2),
         )
 
@@ -1327,12 +1340,31 @@
             normed.at[i],
             spot(i, place),
             plane_send.at[i, 0],
-            plane_recv.at[i // 2, place],
+            plane_recv.at[i // 2, place, 0],
             seq=partner,
         )
 
     def to_self(i):
         return pltpu.make_async_copy(normed.at[i], spot(i, place), plane_send.at[i, 0])
+
+    def relay(i, k, core):
+        at = (across, along)[k] * 2 + core
+        return remote(
+            spot(i, at, k),
+            spot(i, at, k),
+            relay_send.at[i // 2, k, core],
+            plane_recv.at[i // 2, at, k],
+            mp=(along, across)[k],
+        )
+
+    def forward(i):
+        @pl.when(lax.rem(i, 2) == c)
+        def _():
+            for k in range(2):
+                for core in range(2):
+                    at = (across, along)[k] * 2 + core
+                    landed(spot(i, at), plane_recv.at[i // 2, at, 0])
+                    relay(i, k, core).start()
 
     def finish(i):
         for k in range(1, per):
@@ -1345,8 +1377,8 @@
             here = slice(sub * QB, (sub + 1) * QB)
             scale = lax.rsqrt(column[here, 0:1] / (per * inner) + 1e-05)
             normed[i, here, :] = (out[i, here, :].astype(F32) * scale * gain_ref[...]).astype(BF16)
-        for d in range(1, m):
-            to_plane(i, d).start()
+        for k in range(2):
+            to_plane(i, k).start()
 
         @pl.when(lax.rem(i, 2) == c)
         def _():
@@ -1434,27 +1466,39 @@
         for k in range(1, per):
             tell(i, k).start()
 
-        @pl.when(i == n // 2)
+        @pl.when(i < parts)
+        def _():
+            for d in range(1, chips):
+                first_leg(d, i).start()
+
+        @pl.when(i > 1)
+        def _():
+            forward(i - 2)
+
+        @pl.when(i == n - 3)
         def _():
             keep_held().wait()
             for d in range(1, chips):
-                landed(held_ref.at[lax.rem(z + d, chips)], wout_recv.at[0, chips - d])
+                for q in range(parts):
+                    landed(
+                        held_ref.at[lax.rem(z + d, chips), q * slim : (q + 1) * slim, :],
+                        first_recv.at[q, chips - d],
+                    )
             keep_rows().start()
             for d in range(1, m):
                 second_leg(d).start()
 
-        @pl.when(i == n - 2)
-        def _():
-            keep_rows().wait()
-            third_leg(0).start()
-            for d in range(1, m):
-                landed(second_place(lax.rem(member + d, m)), wout_recv.at[1, m - d])
-                third_leg(d).start()
-
         return carry_none
 
     lax.fori_loop(0, n, block, 0)
     finish(n - 1)
+    forward(n - 2)
+    keep_rows().wait()
+    third_leg(0).start()
+    for d in range(1, m):
+        landed(second_place(lax.rem(member + d, m)), wout_recv.at[1, m - d])
+        third_leg(d).start()
+    forward(n - 1)
     for d in range(m):
         strips = pl.ds(pl.multiple_of((1 - c) * strip, strip), strip)
         of = lax.rem(member + d, m)
@@ -1463,17 +1507,19 @@
             wout_recv.at[2, d],
         )
     for j in range(chips):
-        for at in range(2 * m):
-
-            @pl.when(at != place)
-            def _():
-                landed(y_ref.at[j, :, at * inner : (at + 1) * inner], plane_recv.at[j, at])
+        at = member * 2 + 1 - c
+        landed(spot(2 * j, at), plane_recv.at[j, at, 0])
+        for half in range(2):
+            for core in range(2):
+                at = far * 2 + core
+                landed(spot(2 * j, at, half), plane_recv.at[j, at, half])
+                relay(2 * j, half, core).wait_send()
 
     def flush(i, carry_none):
         for k in range(1, per):
             tell(i, k).wait_send()
-        for d in range(1, m):
-            to_plane(i, d).wait_send()
+        for k in range(2):
+            to_plane(i, k).wait_send()
 
         @pl.when(lax.rem(i, 2) == c)
         def _():
@@ -1487,7 +1533,8 @@
 
     lax.fori_loop(0, n, flush, 0)
     for d in range(1, chips):
-        first_leg(d).wait_send()
+        for q in range(parts):
+            first_leg(d, q).wait_send()
     for d in range(1, m):
         second_leg(d).wait_send()
     for d in range(m):
@@ -1507,13 +1554,13 @@
     return pl.pallas_call(
         functools.partial(heads_kernel, n, groups),
         out_shape=(
-            jax.ShapeDtypeStruct((n // 2, rows, 2 * m * inner), BF16),
+            jax.ShapeDtypeStruct((n // 2, 2 * m, rows, inner), BF16),
             jax.ShapeDtypeStruct((m * quarter, 2 * strip), BF16),
-            jax.ShapeDtypeStruct((n // 2, quarter, strip), BF16),
         ),
         in_specs=[anywhere] + [vmem] * 7 + [anywhere],
-        out_specs=(anywhere,) * 3,
+        out_specs=(anywhere, vmem),
         scratch_shapes=[
+            pltpu.VMEM((n // 2, quarter, strip), BF16),
             pltpu.VMEM((2, rows, features), BF16),
             pltpu.VMEM((LANES, features), BF16),
             pltpu.VMEM((8 + rows, width), F32),
@@ -1528,8 +1575,11 @@
             pltpu.SemaphoreType.DMA((2,)),
             pltpu.SemaphoreType.DMA((n, per)),
             pltpu.SemaphoreType.DMA((n, per)),
-            pltpu.SemaphoreType.DMA((n, m)),
-            pltpu.SemaphoreType.DMA((n // 2, 2 * m)),
+            pltpu.SemaphoreType.DMA((n, 3)),
+            pltpu.SemaphoreType.DMA((n // 2, 2 * m, 2)),
+            pltpu.SemaphoreType.DMA((n // 2, 2, 2)),
+            pltpu.SemaphoreType.DMA((n // 2, n // 2)),
+            pltpu.SemaphoreType.DMA((n // 2, n // 2)),
             pltpu.SemaphoreType.DMA((3, m)),
             pltpu.SemaphoreType.DMA((3, m)),
         ],
@@ -1568,8 +1618,8 @@
     along = lax.rem(member + 2, 4)
     far = 3 - member
     rows, wide = hidden_ref.shape
-    tile = part.shape[1]
-    tiles = wide // tile
+    tall = part.shape[0]
+    chunks = rows // tall
     has_up, has_down = z + 1 <= chips - 1, z >= 1
 
     barrier = pltpu.get_barrier_semaphore()
@@ -1594,128 +1644,163 @@
     def _():
         pl.semaphore_wait(barrier, 3)
 
-    def hand_on(j, t, way):
-        here = slice(t * tile, (t + 1) * tile)
+    def span(r):
+        return pl.ds(pl.multiple_of(r * tall, tall), tall)
+
+    def hand_on(j, r, way):
         return pltpu.make_async_remote_copy(
-            src_ref=outgoing.at[j, :, here],
-            dst_ref=incoming.at[way, j, :, here],
-            send_sem=send_sem.at[j, t],
-            recv_sem=recv_sem.at[way, j, t],
+            src_ref=outgoing.at[j, span(r), :],
+            dst_ref=incoming.at[way, j, span(r), :],
+            send_sem=send_sem.at[j, r],
+            recv_sem=recv_sem.at[way, j, r],
             device_id={"seq": me + 2 if way == 0 else me - 2},
             device_id_type=pl.DeviceIdType.MESH,
         )
 
-    def take(j, t, way):
-        here = slice(t * tile, (t + 1) * tile)
-        where = incoming.at[way, j, :, here]
-        pltpu.make_async_copy(where, where, recv_sem.at[way, j, t]).wait()
-        return incoming[way, j, :, here].astype(F32)
+    def take(j, r, way):
+        where = incoming.at[way, j, span(r), :]
+        pltpu.make_async_copy(where, where, recv_sem.at[way, j, r]).wait()
+        return incoming[way, j, span(r), :].astype(F32)
+
+    def feature(owner, r, half=None):
+        at = pl.ds(pl.multiple_of(owner * wide, wide), wide)
+        if half is None:
+            return normed_ref.at[span(r), at]
+        size = tall // 2
+        return normed_ref.at[pl.ds(pl.multiple_of(r * tall + half * size, size), size), at]
+
+    def shares(r):
+        return [
+            pltpu.make_async_remote_copy(
+                src_ref=source,
+                dst_ref=place,
+                send_sem=mp_send.at[r, index],
+                recv_sem=mp_recv.at[r, index],
+                device_id={"mp": target},
+                device_id_type=pl.DeviceIdType.MESH,
+            )
+            for index, (source, place, target) in enumerate(
+                (
+                    (low.at[span(r), :], feature(member, r), across),
+                    (low.at[span(r), :], feature(member, r), along),
+                    (feature(across, r, 0), feature(across, r, 0), along),
+                    (feature(along, r, 1), feature(along, r, 1), across),
+                )
+            )
+        ]
+
+    def own_copy(r):
+        return pltpu.make_async_copy(low.at[span(r), :], feature(member, r), own_sem.at[r])
+
+    def arrived(r, index, place):
+        pltpu.make_async_copy(place, place, mp_recv.at[r, index]).wait()
+
+    def relay(r):
+        mine = shares(r)
+        arrived(r, 0, feature(across, r))
+        mine[2].start()
+        arrived(r, 1, feature(along, r))
+        mine[3].start()
+
+    def settle(r):
+        arrived(r, 2, feature(far, r, 0))
+        arrived(r, 3, feature(far, r, 1))
+        own_copy(r).wait()
+        for copy in shares(r):
+            copy.wait_send()
+        step = min(64, tall)
+        for at in range(0, tall, step):
+            here = pl.ds(pl.multiple_of(r * tall + at, step), step)
+            normed_ref[here, :] = rms_norm(
+                normed_ref[here, :].astype(F32), gain_ref[...]
+            ).astype(BF16)
 
     order = []
     for k in range((chips + 1) // 2):
         order += [chips - 1 - k] + ([k] if k != chips - 1 - k else [])
-    for j in order:
-        for t in range(tiles):
-            here = slice(t * tile, (t + 1) * tile)
+
+    def product(j, r):
+        y = jnp.concatenate([y_ref[j, at, span(r), :] for at in range(y_ref.shape[1])], axis=1)
+        return jnp.dot(y, w_ref[...], preferred_element_type=F32)
+
+    def outward(r):
+        for j in order:
 
             @pl.when(z != j)
             def _():
-                part[...] = jnp.dot(y_ref[j], w_ref[:, here], preferred_element_type=F32)
+                part[...] = product(j, r)
 
             @pl.when(jnp.logical_and(z < j, z >= 1))
             def _():
-                part[...] += take(j, t, 0)
+                part[...] += take(j, r, 0)
 
             @pl.when(jnp.logical_and(z > j, z <= chips - 2))
             def _():
-                part[...] += take(j, t, 1)
+                part[...] += take(j, r, 1)
 
             @pl.when(z != j)
             def _():
-                outgoing[j, :, here] = part[...].astype(BF16)
+                outgoing[j, span(r), :] = part[...].astype(BF16)
 
             @pl.when(z < j)
             def _():
-                hand_on(j, t, 0).start()
+                hand_on(j, r, 0).start()
 
             @pl.when(z > j)
             def _():
-                hand_on(j, t, 1).start()
-
-    for t in range(tiles):
-        here = slice(t * tile, (t + 1) * tile)
-        mixed_ref[:, here] = hidden_ref[:, here].astype(F32) + jnp.dot(
-            y_ref[z], w_ref[:, here], preferred_element_type=F32
-        )
-    for t in range(tiles):
-        here = slice(t * tile, (t + 1) * tile)
+                hand_on(j, r, 1).start()
+
+    def final(r):
+        part[...] = hidden_ref[span(r), :].astype(F32) + product(z, r)
 
         @pl.when(has_down)
         def _():
-            mixed_ref[:, here] += take(z, t, 0)
+            part[...] += take(z, r, 0)
 
         @pl.when(has_up)
         def _():
-            mixed_ref[:, here] += take(z, t, 1)
-
-        low[:, here] = mixed_ref[:, here].astype(BF16)
-
-    def feature(owner, half=None):
-        at = pl.ds(pl.multiple_of(owner * wide, wide), wide)
-        if half is None:
-            return normed_ref.at[:, at]
-        return normed_ref.at[half * (rows // 2) : (half + 1) * (rows // 2), at]
-
-    def share(index, source, place, target):
-        return pltpu.make_async_remote_copy(
-            src_ref=source,
-            dst_ref=place,
-            send_sem=mp_send.at[index],
-            recv_sem=mp_recv.at[index],
-            device_id={"mp": target},
-            device_id_type=pl.DeviceIdType.MESH,
-        )
-
-    def arrived(index, place):
-        pltpu.make_async_copy(place, place, mp_recv.at[index]).wait()
-
-    shared = [
-        share(0, low, feature(member), across),
-        share(1, low, feature(member), along),
-        share(2, feature(across, 0), feature(across, 0), along),
-        share(3, feature(along, 1), feature(along, 1), across),
-    ]
-    shared[0].start()
-    shared[1].start()
-    own_copy = pltpu.make_async_copy(low, feature(member), own_sem)
-    own_copy.start()
-    arrived(0, feature(across))
-    shared[2].start()
-    arrived(1, feature(along))
-    shared[3].start()
-    arrived(2, feature(far, 0))
-    arrived(3, feature(far, 1))
-    own_copy.wait()
-    for copy in shared:
-        copy.wait_send()
-    norm_rows(normed_ref, gain_ref, normed_ref)
-    for j in range(chips):
-        for t in range(tiles):
+            part[...] += take(z, r, 1)
+
+        mixed_ref[span(r), :] = part[...]
+        low[span(r), :] = part[...].astype(BF16)
+        mine = shares(r)
+        mine[0].start()
+        mine[1].start()
+        own_copy(r).start()
+
+    def chunk(r, carry_none):
+        for lag, stage in enumerate((outward, final, relay, settle)):
+
+            @pl.when(jnp.logical_and(r >= lag, r < chunks + lag))
+            def _():
+                stage(r - lag)
+
+        return carry_none
+
+    lax.fori_loop(0, chunks + 3, chunk, 0)
+
+    def flush(r, carry_none):
+        for j in range(chips):
 
             @pl.when(z < j)
             def _():
-                hand_on(j, t, 0).wait_send()
+                hand_on(j, r, 0).wait_send()
 
             @pl.when(z > j)
             def _():
-                hand_on(j, t, 1).wait_send()
+                hand_on(j, r, 1).wait_send()
+
+        return carry_none
+
+    lax.fori_loop(0, chunks, flush, 0)
 
 
 def combine(y, weights, hidden, gain):
     n = lax.axis_size("seq")
     rows, wide = hidden.shape
     chips = n // 2
-    tile = min(256, wide)
+    tall = min(128, rows)
+    chunks = rows // tall
     vmem = pl.BlockSpec(memory_space=pltpu.VMEM)
     return pl.pallas_call(
         functools.partial(combine_kernel, n),
@@ -1726,15 +1811,15 @@
         in_specs=[vmem] * 4,
         out_specs=(vmem, vmem),
         scratch_shapes=[
-            pltpu.VMEM((rows, tile), F32),
+            pltpu.VMEM((tall, wide), F32),
             pltpu.VMEM((chips, rows, wide), BF16),
             pltpu.VMEM((2, chips, rows, wide), BF16),
             pltpu.VMEM((rows, wide), BF16),
-            pltpu.SemaphoreType.DMA((chips, wide // tile)),
-            pltpu.SemaphoreType.DMA((2, chips, wide // tile)),
-            pltpu.SemaphoreType.DMA,
-            pltpu.SemaphoreType.DMA((4,)),
-            pltpu.SemaphoreType.DMA((4,)),
+            pltpu.SemaphoreType.DMA((chips, chunks)),
+            pltpu.SemaphoreType.DMA((2, chips, chunks)),
+            pltpu.SemaphoreType.DMA((chunks,)),
+            pltpu.SemaphoreType.DMA((chunks, 4)),
+            pltpu.SemaphoreType.DMA((chunks, 4)),
         ],
         compiler_params=pltpu.CompilerParams(
             collective_id=6, has_side_effects=True, vmem_limit_bytes=56 * 1024 * 1024
@@ -1818,7 +1903,7 @@
             hidden_in, norm_gain, w_z, w_x, w_b, w_c, w_dt, conv_x, conv_b, conv_c, dt_bias,
             a_rate, skip_gain, group_gain,
         )
-        y_normed, out_rows, _ = mix(hidden, w_out)
+        y_normed, out_rows = mix(hidden, w_out)
         mixed, normed_two = combine(y_normed, out_rows, hidden_in, attn_gain[None, :])
     else:
         proj = gather_dot(

time: 536 us -> 471 us (0.88)
  Pallas kernels: 520 us -> 455 us
    pallas_call x1, Pallas kernels: 156 us -> 117 us  [mix_heads(): pl.pallas_call(functools.partial(heads_kernel, n, groups), out_shape=(jax...]
    pallas_call x1, Pallas kernels: 100 us -> 68.2 us  [line_attention(): pl.pallas_call(functools.partial(line_attention_kernel, n), out_shape=jax...]
    pallas_call x1, Pallas kernels: 86.1 us -> 93.7 us  [combine(): pl.pallas_call(functools.partial(combine_kernel, n), out_shape=(jax.Shape...]
where the time goes in v3:
time: 471 us
  Pallas kernels  455 us (97%)
  local copies, waits for them, and re-layouts  14.6 us (3%)
    pallas_call x1, Pallas kernels, spread(): pl.pallas_call(functools.partial(spread_kernel, n, groups), out_shape=(ja...  177 us
    pallas_call x1, Pallas kernels, mix_heads(): pl.pallas_call(functools.partial(heads_kernel, n, groups), out_shape=(jax...  117 us
    pallas_call x1, Pallas kernels, combine(): pl.pallas_call(functools.partial(combine_kernel, n), out_shape=(jax.Shape...  93.7 us
    pallas_call x1, Pallas kernels, line_attention(): pl.pallas_call(functools.partial(line_attention_kernel, n), out_shape=jax...  68.2 us
    unnamed x22, local copies, waits for them, and re-layouts  9.57 us

profile of v3, /device:TPU:25, one launch (start us, length us, event | category | flops | bytes accessed | tf_op | source)
XLA Modules:
  0.0 470.9 jit_solution(13789451557310880611)
XLA Ops:
  0.6 0.0 copy-start
  0.6 0.0 copy-start.2
  0.7 0.0 copy-start.6
  0.7 0.8 dynamic-slice.18
  1.5 0.7 dynamic-slice_bitcast_fusion
  2.3 0.8 dynamic-slice.19
  3.0 0.1 broadcast_in_dim.6
  3.1 0.1 broadcast_in_dim.14.skip_ref
  3.2 0.0 copy-done
  3.2 0.7 dynamic-slice.15
  3.9 0.7 constant_dynamic-slice_fusion
  4.6 1.1 fusion
  5.7 0.1 pad_maximum_fusion.wbc_ref
  5.8 0.0 copy-done.2
  5.8 0.0 copy-done.6
  5.8 0.0 copy-start.3
  5.8 1.6 copy-done.3
  7.4 0.0 copy-start.4
  7.4 1.6 copy-done.4
  9.0 0.0 copy-start.5
  9.0 176.7 %shard_map.194 = (bf16[4096,4096]{1,0:T(8,128)(2,1)}, bf16[4096,768]{1,0:T(8,128)(2,1)S(1)}, bf16[32,4096]{1,0:T(8,128)(2,1)S(1)}) custom-call(bf16[512,1024]{1,0:T(8,128)(2,1)S(1)} %copy-done.2, f32[1,1024]{1,0:T(1,128)S(1)} %bitcast.8, bf16[512,2048]{1,0:T(8,128)(2,1)S(1)} %copy-done.3, bf16[512,2048]{1,0:T(8,128)(2,1)S(1)} %copy-done.4, ...), custom_call_target="tpu_custom_call" | custom-call | flops 20000000000 | bytes 100000000 | tf_op jit(solution)/shard_map/pallas_call | solution.py:1140
  185.7 0.0 copy-start.7
  185.7 2.7 copy-done.7
  188.4 0.0 copy-done.5
  188.4 116.9 %shard_map.195 = (bf16[4,8,512,256]{3,2,1,0:T(8,128)(2,1)}, bf16[2048,1024]{1,0:T(8,128)(2,1)}) custom-call(bf16[4096,4096]{1,0:T(8,128)(2,1)} %get-tuple-element.9.hidden_ref, bf16[4096,768]{1,0:T(8,128)(2,1)} %copy-done.7, bf16[32,4096]{1,0:T(8,128)(2,1)S(1)} %get-tuple-element.11.wdt_ref, f32[4,512]{1,0:T(4,128)S(1)} %pad_maximum_fusion.1.taps_ref, ...), custom_call_target="tpu_custom_call" | custom-call | flops 40000000000 | bytes 50000000 | tf_op jit(solution)/shard_map/pallas_call | solution.py:1554
  305.3 93.7 %shard_map.196 = (f32[512,1024]{1,0:T(8,128)}, bf16[512,4096]{1,0:T(8,128)(2,1)}) custom-call(bf16[4,8,512,256]{3,2,1,0:T(8,128)(2,1)} %get-tuple-element.12.y_ref, bf16[2048,1024]{1,0:T(8,128)(2,1)} %get-tuple-element.13.w_ref, bf16[512,1024]{1,0:T(8,128)(2,1)} %hidden_ref.3, f32[1,4096]{1,0:T(1,128)} %bitcast.11), custom_call_target="tpu_custom_call" | custom-call | flops 2147483648 | bytes 60000000 | tf_op jit(solution)/shard_map/pallas_call | solution.py:1805
  399.0 0.0 copy-start.8
  399.0 68.2 %shard_map.197 = f32[512,1024]{1,0:T(8,128)} custom-call(bf16[512,4096]{1,0:T(8,128)(2,1)} %get-tuple-element.15.nt_ref, bf16[4096,1024]{1,0:T(8,128)(2,1)} %wq_ref.1, bf16[4096,256]{1,0:T(8,128)(2,1)} %wk_ref.1, bf16[4096,256]{1,0:T(8,128)(2,1)} %wv_ref.1), custom_call_target="tpu_custom_call" | custom-call | flops 17999998976 | bytes 30000000 | tf_op jit(solution)/shard_map/pallas_call | solution.py:836
  467.2 0.0 copy-done.8
  467.3 0.0 copy-start.9
  467.3 0.0 copy-start.1
  467.3 1.3 copy.23
  468.6 1.0 copy-done.9
  469.6 1.3 copy.24
  470.9 0.0 copy-done.1
  (4 shorter events, 0.0 us)
Async XLA Ops:
  0.6 2.6 copy-start
  0.6 5.1 %copy-start.2 = (bf16[512,1024]{1,0:T(8,128)(2,1)S(1)}, bf16[512,1024]{1,0:T(8,128)(2,1)}, u32[]{:S(2)}) copy-start(bf16[512,1024]{1,0:T(8,128)(2,1)} %hidden_ref.3) | copy-start | bytes 3145732
  0.7 5.1 %copy-start.6 = (bf16[512,32]{0,1:T(8,128)(2,1)S(1)}, bf16[512,32]{0,1:T(8,128)(2,1)}, u32[]{:S(2)}) copy-start(bf16[512,32]{0,1:T(8,128)(2,1)} %param.25) | copy-start | bytes 98308
  5.8 1.6 copy-start.3
  7.4 1.6 copy-start.4
  9.0 179.4 %copy-start.5 = (bf16[2048,512]{1,0:T(8,128)(2,1)S(1)}, bf16[2048,512]{1,0:T(8,128)(2,1)}, u32[]{:S(2)}) copy-start(bf16[2048,512]{1,0:T(8,128)(2,1)} %wout_ref.1) | copy-start | bytes 6291460
  185.7 2.7 copy-start.7
  399.0 68.2 %copy-start.8 = (f32[512,1024]{1,0:T(8,128)S(1)}, f32[512,1024]{1,0:T(8,128)}, u32[]{:S(2)}) copy-start(f32[512,1024]{1,0:T(8,128)} %get-tuple-element.28) | copy-start | bytes 6291460
  467.3 2.3 copy-start.9
  467.3 3.7 copy-start.1

commit v4 on v3

--- a/solution.py
+++ b/solution.py
@@ -1007,9 +1007,10 @@
     def normalise(i, carry):
         at = pl.ds(pl.multiple_of(i * tile, tile), tile)
         scale = lax.rsqrt(cols[at, 0:1] / (4 * wide) + 1e-05)
-        own[at, :] = (hidden_ref[at, :].astype(F32) * scale * gain_ref[...]).astype(BF16)
+        own[at, :] = (hidden_ref[at, :].astype(F32) * scale * gain).astype(BF16)
         return carry
 
+    gain = gain_ref[:, pl.ds(pl.multiple_of(member * wide, wide), wide)]
     lax.fori_loop(0, rows // tile, normalise, 0)
 
     def valid(slot):
@@ -1169,7 +1170,9 @@
     hidden_ref,
     w_ref,
     wdt_ref,
-    taps_ref,
+    cx_ref,
+    cb_ref,
+    cc_ref,
     bias_ref,
     rate_ref,
     skip_ref,
@@ -1178,6 +1181,7 @@
     y_ref,
     rows_ref,
     held_ref,
+    taps_ref,
     blocks,
     wdt_own,
     window,
@@ -1294,6 +1298,11 @@
         )
 
     load(0, 0).start()
+    shared = pl.ds(pl.multiple_of(me * groups // n * N, N), N)
+    taps_ref[:, 0:inner] = cx_ref[:, pl.ds(pl.multiple_of(me * inner, inner), inner)]
+    taps_ref[:, inner : inner + N] = cb_ref[:, shared]
+    taps_ref[:, inner + N : width] = cc_ref[:, shared]
+    own_gain = gain_ref[:, pl.ds(pl.multiple_of(me * inner, inner), inner)]
     all_heads = wdt_ref.shape[0]
     pick_row = lax.broadcasted_iota(jnp.int32, (LANES, all_heads), 0)
     pick_col = lax.broadcasted_iota(jnp.int32, (LANES, all_heads), 1)
@@ -1376,7 +1385,7 @@
         for sub in range(rows // QB):
             here = slice(sub * QB, (sub + 1) * QB)
             scale = lax.rsqrt(column[here, 0:1] / (per * inner) + 1e-05)
-            normed[i, here, :] = (out[i, here, :].astype(F32) * scale * gain_ref[...]).astype(BF16)
+            normed[i, here, :] = (out[i, here, :].astype(F32) * scale * own_gain).astype(BF16)
         for k in range(2):
             to_plane(i, k).start()
 
@@ -1557,10 +1566,11 @@
             jax.ShapeDtypeStruct((n // 2, 2 * m, rows, inner), BF16),
             jax.ShapeDtypeStruct((m * quarter, 2 * strip), BF16),
         ),
-        in_specs=[anywhere] + [vmem] * 7 + [anywhere],
+        in_specs=[anywhere] + [vmem] * 9 + [anywhere],
         out_specs=(anywhere, vmem),
         scratch_shapes=[
             pltpu.VMEM((n // 2, quarter, strip), BF16),
+            pltpu.VMEM((taps[0].shape[0], width), F32),
             pltpu.VMEM((2, rows, features), BF16),
             pltpu.VMEM((LANES, features), BF16),
             pltpu.VMEM((8 + rows, width), F32),
@@ -1589,7 +1599,7 @@
         cost_estimate=pl.CostEstimate(
             flops=40_000_000_000, bytes_accessed=50_000_000, transcendentals=8_000_000
         ),
-    )(hidden, weights, w_dt, taps, bias, rate, skip, gain, w_out)
+    )(hidden, weights, w_dt, *taps, bias, rate, skip, gain, w_out)
 
 
 def combine_kernel(
@@ -1845,27 +1855,21 @@
     groups = conv_b.shape[1] // N
     inner = conv_x.shape[1] // n
     heads = dt_bias.shape[0] // n
-    group = me * groups // n
     pieces = []
     for g in range(groups):
         pieces += [w_b[:, g * N : (g + 1) * N], w_c[:, g * N : (g + 1) * N]]
-    gain = own_slice(norm_gain[None, :], lax.axis_index("mp"), hidden_in.shape[1])
     hidden, weights, steps = spread(
-        hidden_in, gain, w_x, w_z, jnp.concatenate(pieces, axis=1), jnp.transpose(w_dt), groups
-    )
-    taps = jnp.concatenate(
-        [own_slice(conv_x, me, inner), own_slice(conv_b, group, N), own_slice(conv_c, group, N)],
-        axis=1,
+        hidden_in, norm_gain[None, :], w_x, w_z, jnp.concatenate(pieces, axis=1), jnp.transpose(w_dt), groups
     )
     return hidden, functools.partial(
         mix_heads,
         weights=weights,
         w_dt=steps,
-        taps=taps,
+        taps=(conv_x, conv_b, conv_c),
         bias=pad_lanes(own_slice(dt_bias[None, :], me, heads)),
         rate=pad_lanes(own_slice(a_rate[None, :], me, heads)),
         skip=jnp.repeat(own_slice(skip_gain[None, :], me, heads), P_SIZE, axis=1),
-        gain=own_slice(group_gain[None, :], me, inner),
+        gain=group_gain[None, :],
         groups=groups,
     )
 

time: 471 us -> 470 us (level)
    unnamed x22 -> x28, local copies, waits for them, and re-layouts: 9.57 us -> 9.59 us
where the time goes in v4:
time: 470 us; the launch traced here: 469 us
  Pallas kernels  456 us (97%)
  local copies, waits for them, and re-layouts  12.4 us (3%)
    pallas_call x1, Pallas kernels, spread(): pl.pallas_call(functools.partial(spread_kernel, n, groups), out_shape=(ja...  177 us
    pallas_call x1, Pallas kernels, mix_heads(): pl.pallas_call(functools.partial(heads_kernel, n, groups), out_shape=(jax...  118 us
    pallas_call x1, Pallas kernels, combine(): pl.pallas_call(functools.partial(combine_kernel, n), out_shape=(jax.Shape...  93.2 us
    pallas_call x1, Pallas kernels, line_attention(): pl.pallas_call(functools.partial(line_attention_kernel, n), out_shape=jax...  68.3 us
    unnamed x28, local copies, waits for them, and re-layouts  9.59 us

profile of v4, /device:TPU:25, one launch (start us, length us, event | category | flops | bytes accessed | tf_op | source)
XLA Modules:
  0.0 469.3 jit_solution(8881674429586747089)
XLA Ops:
  0.6 0.0 copy-start
  0.6 0.0 copy-start.4
  0.7 0.0 copy-start.6
  0.7 0.8 dynamic-slice.11
  1.5 0.7 dynamic-slice_bitcast_fusion
  2.2 0.1 broadcast_in_dim.18
  2.3 0.1 broadcast_in_dim.19.skip_ref
  2.4 1.1 fusion
  3.5 0.1 pad_maximum_fusion.wbc_ref
  3.6 0.0 copy-done
  3.6 0.0 copy-done.4
  3.6 0.0 copy-done.6
  3.6 0.0 copy-start.1
  3.6 1.6 copy-done.1
  5.2 0.0 copy-start.2
  5.2 1.6 copy-done.2
  6.8 0.0 copy-start.3
  6.8 0.0 copy-start.5
  6.8 0.0 copy-start.7
  6.8 0.0 copy-start.8
  6.8 0.0 copy-start.9
  6.8 176.8 %shard_map.194 = (bf16[4096,4096]{1,0:T(8,128)(2,1)}, bf16[4096,768]{1,0:T(8,128)(2,1)S(1)}, bf16[32,4096]{1,0:T(8,128)(2,1)S(1)}) custom-call(bf16[512,1024]{1,0:T(8,128)(2,1)S(1)} %copy-done, f32[1,4096]{1,0:T(1,128)S(1)} %bitcast.9, bf16[512,2048]{1,0:T(8,128)(2,1)S(1)} %copy-done.1, bf16[512,2048]{1,0:T(8,128)(2,1)S(1)} %copy-done.2, ...), custom_call_target="tpu_custom_call" | custom-call | flops 20000000000 | bytes 100000000 | tf_op jit(solution)/shard_map/pallas_call | solution.py:1141
  183.7 0.0 copy-start.10
  183.7 2.7 copy-done.10
  186.4 0.0 copy-done.3
  186.4 0.0 copy-done.5
  186.4 0.0 copy-done.7
  186.4 0.0 copy-done.8
  186.4 0.0 copy-done.9
  186.4 117.8 %shard_map.195 = (bf16[4,8,512,256]{3,2,1,0:T(8,128)(2,1)}, bf16[2048,1024]{1,0:T(8,128)(2,1)}) custom-call(bf16[4096,4096]{1,0:T(8,128)(2,1)} %get-tuple-element.9.hidden_ref, bf16[4096,768]{1,0:T(8,128)(2,1)} %copy-done.10, bf16[32,4096]{1,0:T(8,128)(2,1)S(1)} %get-tuple-element.11.wdt_ref, f32[4,2048]{1,0:T(4,128)S(1)} %copy-done.5, ...), custom_call_target="tpu_custom_call" | custom-call | flops 40000000000 | bytes 50000000 | tf_op jit(solution)/shard_map/pallas_call | solution.py:1563
  304.2 93.2 %shard_map.196 = (f32[512,1024]{1,0:T(8,128)}, bf16[512,4096]{1,0:T(8,128)(2,1)}) custom-call(bf16[4,8,512,256]{3,2,1,0:T(8,128)(2,1)} %get-tuple-element.12.y_ref, bf16[2048,1024]{1,0:T(8,128)(2,1)} %get-tuple-element.13.w_ref, bf16[512,1024]{1,0:T(8,128)(2,1)} %hidden_ref.3, f32[1,4096]{1,0:T(1,128)} %bitcast.11), custom_call_target="tpu_custom_call" | custom-call | flops 2147483648 | bytes 60000000 | tf_op jit(solution)/shard_map/pallas_call | solution.py:1815
  397.4 0.0 copy-start.11
  397.4 68.3 %shard_map.197 = f32[512,1024]{1,0:T(8,128)} custom-call(bf16[512,4096]{1,0:T(8,128)(2,1)} %get-tuple-element.15.nt_ref, bf16[4096,1024]{1,0:T(8,128)(2,1)} %wq_ref.1, bf16[4096,256]{1,0:T(8,128)(2,1)} %wk_ref.1, bf16[4096,256]{1,0:T(8,128)(2,1)} %wv_ref.1), custom_call_target="tpu_custom_call" | custom-call | flops 17999998976 | bytes 30000000 | tf_op jit(solution)/shard_map/pallas_call | solution.py:836
  465.7 0.0 copy-done.11
  465.7 0.0 copy-start.12
  465.7 1.3 copy.23
  467.0 1.0 copy-done.12
  468.0 1.3 copy.24
  (2 shorter events, 0.0 us)
Async XLA Ops:
  0.6 3.0 copy-start
  0.6 3.0 copy-start.4
  0.7 3.0 copy-start.6
  3.6 1.6 copy-start.1
  5.2 1.6 copy-start.2
  6.8 179.6 %copy-start.3 = (bf16[2048,512]{1,0:T(8,128)(2,1)S(1)}, bf16[2048,512]{1,0:T(8,128)(2,1)}, u32[]{:S(2)}) copy-start(bf16[2048,512]{1,0:T(8,128)(2,1)} %wout_ref.1) | copy-start | bytes 6291460
  6.8 179.6 %copy-start.5 = (f32[4,2048]{1,0:T(4,128)S(1)}, f32[4,2048]{1,0:T(4,128)}, u32[]{:S(2)}) copy-start(f32[4,2048]{1,0:T(4,128)} %cx_ref.1) | copy-start | bytes 98308
  6.8 179.6 %copy-start.7 = (f32[2048]{0:T(1024)S(1)}, f32[2048]{0:T(1024)}, u32[]{:S(2)}) copy-start(f32[2048]{0:T(1024)} %param.32) | copy-start | bytes 24580
  6.8 179.6 %copy-start.8 = (f32[4,256]{1,0:T(4,128)S(1)}, f32[4,256]{1,0:T(4,128)}, u32[]{:S(2)}) copy-start(f32[4,256]{1,0:T(4,128)} %cb_ref.1) | copy-start | bytes 12292
  6.8 179.6 %copy-start.9 = (f32[4,256]{1,0:T(4,128)S(1)}, f32[4,256]{1,0:T(4,128)}, u32[]{:S(2)}) copy-start(f32[4,256]{1,0:T(4,128)} %cc_ref.1) | copy-start | bytes 12292
  183.7 2.7 copy-start.10
  397.4 68.3 %copy-start.11 = (f32[512,1024]{1,0:T(8,128)S(1)}, f32[512,1024]{1,0:T(8,128)}, u32[]{:S(2)}) copy-start(f32[512,1024]{1,0:T(8,128)} %get-tuple-element.26) | copy-start | bytes 6291460
  465.7 2.3 copy-start.12
